TPU v7x, 128 devices: a whole 4x4x4 slice. The times are simulated.
128 devices in a mesh: seq: 16 (over z_lo, y, core), head: 8 (over x, z_hi).
Axes of the slice: x: 4, y: 4, z: 4 (z_hi: 2, z_lo: 2; z = z_hi * 2 + z_lo), core: 2. Of those that a mesh axis runs over, the one named last changes fastest.
Arguments:
- queries: bfloat16 [16, 128, 8192], P('seq', None, 'head'), may hold values from -160 to 160
- continuation_key_slots: bfloat16 [16, 128, 1024], P('seq', None, 'head'), may hold values from -13.1875 to 13.1875
- continuation_value_slots: bfloat16 [16, 128, 1024], P('seq', None, 'head'), may hold values from -24 to 24
- cached_prompt_keys: bfloat16 [2, 16384, 1024], P(None, 'seq', 'head'), may hold values from -6 to 6
- cached_prompt_values: bfloat16 [2, 16384, 1024], P(None, 'seq', 'head'), may hold values from -24 to 24
- pair_lengths: int32 [4, 2], replicated, may hold values from 1 to 256
- prompt_of: int32 [4], replicated, may hold values from 0 to 1
- slot_tile: int32 [16], replicated, may hold values from 0 to 15, each once
- out_weight: bfloat16 [8192, 8192], P('head', 'seq'), may hold values from -0.0625 to 0.0625
Outputs:
- projected: bfloat16 [16, 128, 8192], P('head', None, 'seq')
Inputs may be any that keep to these rules, and one draw needn't show every extreme that they name: `slot_tile`: each of the 16 tiles stands in exactly one slot.
All inputs are finite; a program needn't handle non-finite values.
Results may differ from a plain program's by a relative error of at most 0.014.
Values may be sent and summed in bfloat16 or wider, within the bound.
A program may use at most 128 MiB of HBM per device.

v0:
```python
import math

import jax
import jax.numpy as jnp
from jax import lax
from jax.sharding import PartitionSpec as P

QUERY_HEADS = 64
KEY_VALUE_HEADS = 8
HEAD_WIDTH = 128
TILE_ROWS = 128
MAX_CONT_TILES = 2
PROMPT_COUNT = 2


VERY_LOW = -1e30


def side_by_side(arrays, axis, dim, along):
    widths = [a.shape[along] for a in arrays]
    both = jnp.concatenate(arrays, axis=along)
    result = lax.all_gather(both, axis, axis=dim, tiled=True)
    return tuple(jnp.split(result, [sum(widths[:k]) for k in range(1, len(widths))], axis=along))


def split_up(x, dim, length):
    before, after = (x.shape[:dim], x.shape[dim + 1 :])
    return jnp.moveaxis(x.reshape(*before, length, -1, *after), dim, 0)


def summed_on_arrival(x, axis, dim):
    length = lax.axis_size(axis)
    blocks = lax.all_to_all(split_up(x, dim, length), axis, 0, 0, tiled=True)
    return jnp.sum(blocks.astype(jnp.float32), axis=0)


def tile_scores(query_tile, key_rows):
    raw = jnp.einsum("tkgd,pkd->kgtp", query_tile, key_rows, preferred_element_type=jnp.float32)
    return raw * (1.0 / math.sqrt(query_tile.shape[-1]))


def weigh_values(weights, value_rows):
    return jnp.einsum(
        "kgtp,pkd->kgtd",
        weights.astype(jnp.bfloat16),
        value_rows,
        preferred_element_type=jnp.float32,
    )


def local(
    queries,
    continuation_key_slots,
    continuation_value_slots,
    cached_prompt_keys,
    cached_prompt_values,
    pair_lengths,
    prompt_of,
    slot_tile,
    out_weight,
):
    seq_index = lax.axis_index("seq")
    slot_count = slot_tile.shape[0]
    tiles_here = queries.shape[0]
    kv_local = continuation_key_slots.shape[-1] // HEAD_WIDTH
    heads_per_group = QUERY_HEADS // KEY_VALUE_HEADS
    owner_slot = (
        jnp.zeros((slot_count,), jnp.int32)
        .at[slot_tile]
        .set(jnp.arange(slot_count, dtype=jnp.int32))
    )
    lengths = pair_lengths.reshape(-1)
    prompts = prompt_of[slot_tile // MAX_CONT_TILES // 2]
    local_q = queries.reshape(tiles_here, TILE_ROWS, kv_local, heads_per_group, HEAD_WIDTH)
    own_first = seq_index * tiles_here
    own_prompts = lax.dynamic_slice_in_dim(prompts, own_first, tiles_here, 0)
    start_state = (
        jnp.full((tiles_here, kv_local, heads_per_group, TILE_ROWS), VERY_LOW, jnp.float32),
        jnp.zeros((tiles_here, kv_local, heads_per_group, TILE_ROWS), jnp.float32),
        jnp.zeros((tiles_here, kv_local, heads_per_group, TILE_ROWS, HEAD_WIDTH), jnp.float32),
    )
    piece_keys = lax.all_gather(cached_prompt_keys, "seq", axis=1, tiled=True)
    piece_values = lax.all_gather(cached_prompt_values, "seq", axis=1, tiled=True)
    piece_rows = piece_keys.shape[1]
    block_rows = math.gcd(piece_rows, 1024)

    def one_block(block_id, inner):
        maxima_in, totals_in, weighted_in = inner
        block_keys = lax.dynamic_slice_in_dim(
            piece_keys, block_id * block_rows, block_rows, 1
        ).reshape(PROMPT_COUNT, block_rows, kv_local, HEAD_WIDTH)
        block_values = lax.dynamic_slice_in_dim(
            piece_values, block_id * block_rows, block_rows, 1
        ).reshape(PROMPT_COUNT, block_rows, kv_local, HEAD_WIDTH)
        key_rows = lax.dynamic_index_in_dim(block_keys, own_prompts[0], 0, False)
        value_rows = lax.dynamic_index_in_dim(block_values, own_prompts[0], 0, False)
        scores = tile_scores(local_q[0], key_rows)
        peak_new = jnp.maximum(maxima_in[0], jnp.max(scores, axis=3))
        weights = jnp.exp(scores - peak_new[..., None])
        keep = jnp.exp(maxima_in[0] - peak_new)
        total_new = totals_in[0] * keep + jnp.sum(weights, axis=3)
        weighted_new = weighted_in[0] * keep[..., None] + weigh_values(weights, value_rows)
        updated = [(peak_new, total_new, weighted_new)]
        return (
            jnp.stack([entry[0] for entry in updated]),
            jnp.stack([entry[1] for entry in updated]),
            jnp.stack([entry[2] for entry in updated]),
        )

    maxima, totals, weighted = lax.fori_loop(0, piece_rows // block_rows, one_block, start_state)
    all_keys, all_values = side_by_side(
        (continuation_key_slots, continuation_value_slots), "seq", 0, 1
    )
    slot_index = own_first + 0
    tile_id = slot_tile[slot_index]
    continuation = tile_id // MAX_CONT_TILES
    offset = tile_id % MAX_CONT_TILES * TILE_ROWS
    place_indices = owner_slot[
        continuation * MAX_CONT_TILES + jnp.arange(MAX_CONT_TILES, dtype=jnp.int32)
    ]
    own_keys = all_keys[place_indices].reshape(MAX_CONT_TILES * TILE_ROWS, kv_local, HEAD_WIDTH)
    own_values = all_values[place_indices].reshape(MAX_CONT_TILES * TILE_ROWS, kv_local, HEAD_WIDTH)
    row_pos = offset + jnp.arange(TILE_ROWS, dtype=jnp.int32)
    col_pos = jnp.arange(MAX_CONT_TILES * TILE_ROWS, dtype=jnp.int32)
    causal = col_pos[None, :] <= row_pos[:, None]
    in_length = row_pos < lengths[continuation]
    scores = jnp.where(causal[None, None], tile_scores(local_q[0], own_keys), VERY_LOW)
    peak = jnp.maximum(maxima[0], jnp.max(scores, axis=3))
    weights = jnp.exp(scores - peak[..., None])
    rescale = jnp.exp(maxima[0] - peak)
    denominator = totals[0] * rescale + jnp.sum(weights, axis=3)
    numerator = weighted[0] * rescale[..., None] + weigh_values(weights, own_values)
    result = numerator / denominator[..., None]
    result = jnp.transpose(result, (2, 0, 1, 3)).reshape(
        TILE_ROWS, kv_local * heads_per_group * HEAD_WIDTH
    )
    outputs = [jnp.where(in_length[:, None], result, 0.0).astype(jnp.bfloat16)]
    attention = jnp.stack(outputs)
    partial_out = jnp.einsum(
        "stc,cd->std",
        lax.all_gather(attention, "seq", axis=0, tiled=True),
        out_weight,
        preferred_element_type=jnp.float32,
    )
    projected = summed_on_arrival(partial_out.astype(jnp.bfloat16), "head", 0)
    return projected.astype(jnp.bfloat16)


def solution(mesh):
    return jax.shard_map(
        local,
        mesh=mesh,
        in_specs=(
            P("seq", None, "head"),
            P("seq", None, "head"),
            P("seq", None, "head"),
            P(None, "seq", "head"),
            P(None, "seq", "head"),
            P(),
            P(),
            P(),
            P("head", "seq"),
        ),
        out_specs=P("head", None, "seq"),
        check_vma=False,
    )
```

profile of v0, /device:TPU:48, one launch (start us, length us, event | category | flops | bytes accessed | tf_op | source)
XLA Modules:
  0.0 308.3 jit_solution(1043729643784768387)
XLA Ops:
  22.5 19.4 %all-gather.9.cloned.1.call-done = bf16[16,256,128]{2,1,0:T(8,128)(2,1)} async-done(((bf16[1,256,128]{2,1,0:T(8,128)(2,1)}), bf16[16,256,128]{2,1,0:T(8,128)(2,1)}) %all-gather.9.cloned.1.call-update) | async-done | bytes 1048592 | tf_op jit(solution)/shard_map/all_gather | solution.py:22
  44.6 51.9 %all-gather.5.cloned.1.call-done = bf16[2,16384,128]{2,1,0:T(8,128)(2,1)} async-done(((bf16[2,1024,128]{2,1,0:T(8,128)(2,1)}), bf16[2,16384,128]{2,1,0:T(8,128)(2,1)}) %all-gather.5.cloned.1.call-update) | async-done | bytes 8388624 | tf_op jit(solution)/shard_map/all_gather | solution.py:82
  96.5 54.6 %all-gather.7.cloned.1.call-done = bf16[2,16384,128]{2,1,0:T(8,128)(2,1)} async-done(((bf16[2,1024,128]{2,1,0:T(8,128)(2,1)}), bf16[2,16384,128]{2,1,0:T(8,128)(2,1)}) %all-gather.7.cloned.1.call-update) | async-done | bytes 8388624 | tf_op jit(solution)/shard_map/all_gather | solution.py:83
  151.2 71.7 %while.21 = (s32[]{:T(128)}, f32[1,1,8,128]{3,2,1,0:T(8,128)S(1)}, f32[1,1,8,128]{3,2,1,0:T(8,128)S(1)}, f32[1,1,8,128,128]{4,3,2,1,0:T(8,128)S(1)}, bf16[2,1638...) while((s32[]{:T(128)}, f32[1,1,8,128]{3,2,1,0:T(8,128)S(1)}, ...), condition=%wide.region_3.4_spmd.clone, body=%wide.region_0.3_spmd.clone.sunk | while | flops 545528832 | bytes 15004886 | solution.py:110
  153.7 2.0 fusion.55
  155.8 1.7 bitcast_reduce_fusion.2
  158.2 2.0 fusion.55
  160.2 1.7 bitcast_reduce_fusion.2
  162.6 2.0 fusion.55
  164.7 1.7 bitcast_reduce_fusion.2
  167.1 2.0 fusion.55
  169.2 1.7 bitcast_reduce_fusion.2
  171.6 2.0 fusion.55
  173.7 1.7 bitcast_reduce_fusion.2
  176.1 2.0 fusion.55
  178.2 1.7 bitcast_reduce_fusion.2
  180.6 2.0 fusion.55
  182.6 1.7 bitcast_reduce_fusion.2
  185.0 2.0 fusion.55
  187.1 1.7 bitcast_reduce_fusion.2
  189.5 2.0 fusion.55
  194.0 2.0 fusion.55
  198.5 2.0 fusion.55
  203.0 2.0 fusion.55
  207.4 2.0 fusion.55
  211.9 2.0 fusion.55
  216.4 2.0 fusion.55
  218.5 1.7 bitcast_reduce_fusion.2
  220.9 2.0 fusion.55
  224.6 37.2 %all-gather.11.cloned.1.call-done = bf16[16,128,1024]{2,1,0:T(8,128)(2,1)} async-done(((bf16[1,128,1024]{2,1,0:T(8,128)(2,1)}), bf16[16,128,1024]{2,1,0:T(8,128)(2,1)}) %all-gather.11.cloned.1.call-update) | async-done | bytes 4194320 | tf_op jit(solution)/shard_map/all_gather | solution.py:141
  261.8 4.5 %convolution_convert_fusion = bf16[16,128,512]{2,1,0:T(8,128)(2,1)S(1)} fusion(bf16[16,128,1024]{2,1,0:T(8,128)(2,1)} %all-gather.11.cloned.1.call-done, bf16[1024,512]{1,0:T(8,128)(2,1)S(1)} %copy-done), kind=kOutput, calls=%fused_computation.32 | convolution fusion | flops 2148532224 | bytes 7340032 | tf_op jit(solution)/shard_map/stc,cd->std/dot_general | solution.py:139
  266.3 34.4 %all_to_all.5 = bf16[8,2,128,512]{3,2,1,0:T(8,128)(2,1)S(1)} all-to-all(bf16[8,2,128,512]{3,2,1,0:T(8,128)(2,1)S(1)} %bitcast.139), channel_id=1, replica_groups=mesh['seq'=16,'head'=8] {'head'}, dimensions={0} | all-to-all | bytes 4194304 | tf_op jit(solution)/shard_map/all_to_all | solution.py:33
  (118 shorter events, 40.7 us)
Async XLA Ops:
  6.5 255.3 %copy-start = (bf16[1024,512]{1,0:T(8,128)(2,1)S(1)}, bf16[1024,512]{1,0:T(8,128)(2,1)}, u32[]{:S(2)}) copy-start(bf16[1024,512]{1,0:T(8,128)(2,1)} %param.19) | copy-start | bytes 3145732
  6.5 144.7 %copy-start.1 = (bf16[1,128,1024]{2,1,0:T(8,128)(2,1)S(1)}, bf16[1,128,1024]{2,1,0:T(8,128)(2,1)}, u32[]{:S(2)}) copy-start(bf16[1,128,1024]{2,1,0:T(8,128)(2,1)} %param.11) | copy-start | bytes 786436
  6.5 35.3 %all-gather.9.cloned.1.call-start = ((), (), s32[]{:S(2)}) async-start(), calls=%async_computation.3 | async-start | bytes 1114112 | tf_op jit(solution)/shard_map/all_gather | solution.py:22
  8.1 88.4 %all-gather.5.cloned.1.call-start = ((), (), s32[]{:S(2)}) async-start(), calls=%async_computation.1 | async-start | bytes 8912896 | tf_op jit(solution)/shard_map/all_gather | solution.py:82
  8.8 142.3 %all-gather.7.cloned.1.call-start = ((), (), s32[]{:S(2)}) async-start(), calls=%async_computation.2 | async-start | bytes 8912896 | tf_op jit(solution)/shard_map/all_gather | solution.py:83
  9.6 252.2 %all-gather.11.cloned.1.call-start = ((), (), s32[]{:S(2)}) async-start(), calls=%async_computation.4 | async-start | bytes 4456448 | tf_op jit(solution)/shard_map/all_gather | solution.py:141
Sparse Core Ops, SparseCore 0:
  9.0 32.7 all-gather.8
  43.5 52.9 all-gather.4
  98.2 52.9 all-gather.6
  224.7 37.0 all-gather.10
where the time goes:
time: 312 us; the launch traced here: 308 us
  waiting for transfers between devices  165 us (53%)
  matrix products  63.7 us (20%)
  blocking collectives  34.4 us (11%)
  between operations  17.8 us (6%)
  other arithmetic  16.3 us (5%)
  local copies, waits for them, and re-layouts  10.5 us (3%)
    all_gather x1, waiting for transfers between devices, local(): lax.all_gather(cached_prompt_values, 'seq', axis=1, tiled=True)  54.6 us
    all_gather x1, waiting for transfers between devices, local(): piece_keys = lax.all_gather(cached_prompt_keys, 'seq', axis=1, tiled=True)  51.9 us
    all_gather x1, waiting for transfers between devices, local(): lax.all_gather(attention, 'seq', axis=0, tiled=True)  37.2 us
    all_to_all x1, blocking collectives, summed_on_arrival(): blocks = lax.all_to_all(split_up(x, dim, length), axis, 0, 0, tiled=True)  34.4 us
    dot_general x17, matrix products, weigh_values(): jnp.einsum('kgtp,pkd->kgtd', weights.astype(jnp.bfloat16), value_rows, pr...  32 us
    dot_general x17, matrix products, tile_scores(): jnp.einsum('tkgd,pkd->kgtp', query_tile, key_rows, preferred_element_type...  27.2 us
    all_gather x1, waiting for transfers between devices, side_by_side(): result = lax.all_gather(both, axis, axis=dim, tiled=True)  19.4 us
    reduce_sum x16, other arithmetic, one_block(): total_new = totals_in[0] * keep + jnp.sum(weights, axis=3)  11 us
  transfers between devices with their start and end apart: 4, of which 4 were waited for; matrix products, arithmetic and copies ran while one was open for 4% of the time, Pallas kernels for 0%

commit v1 on v0

v1 whole, which is shorter than its diff:
```python
import functools
import math

import jax
import jax.numpy as jnp
from jax import lax
from jax.experimental import pallas as pl
from jax.experimental.pallas import tpu as pltpu
from jax.sharding import PartitionSpec as P

QUERY_HEADS = 64
KEY_VALUE_HEADS = 8
WIDTH = 128
ROWS = 128
VERY_LOW = -1e30
SCALE = math.log2(math.e) / math.sqrt(WIDTH)
MESH = pl.DeviceIdType.MESH

HEADS_UNIT = 2
UCOLS = HEADS_UNIT * WIDTH
UROWS = HEADS_UNIT * ROWS
CHUNK = 512

PLACES = ((0, 0), (0, 1), (0, 3), (1, 1), (1, 2), (1, 3), (0, 2), (1, 0))
T0, T2, T1, T5, T7, T4, T6, T3 = range(8)
IN67, IN16, IN34, IN35, IN01, IN02, IN03 = range(7)


def across(lhs, rhs):
    return lax.dot_general(lhs, rhs, (((1,), (1,)), ((), ())), preferred_element_type=jnp.float32)


def attend_kernel(
    units,
    lengths, prompts, tiles, q, ck, cv, pk, pv,
    out,
    kall, vall, ckb, cvb, qbuf, obuf, rbuf, lob, lrb, sa, sb, ma, mb, info,
    load_sem, kv_send, kv_recv, q_send, q_recv, o_send, o_recv, l_send, l_recv,
):
    me = lax.axis_index("seq")
    z, y, c = me // 8, (me // 2) % 4, me % 2
    d = 1 - 2 * c
    kd = pk.shape[1]

    def seq(zf, steps):
        return (z + zf) % 2 * 8 + (y + steps * d + 8) % 4 * 2 + c

    def dev(zf, steps):
        return {"seq": seq(zf, steps)}

    other = {"seq": me + d}
    zp, fwd, bwd = dev(1, 0), dev(0, 1), dev(0, -1)

    loads = [
        pltpu.make_async_copy(pk, kall.at[:, pl.ds(0, kd), :], load_sem.at[0]),
        pltpu.make_async_copy(pv, vall.at[:, pl.ds(0, kd), :], load_sem.at[1]),
        pltpu.make_async_copy(ck.at[0], ckb.at[pl.ds(0, ROWS), :], load_sem.at[2]),
        pltpu.make_async_copy(cv.at[0], cvb.at[pl.ds(0, ROWS), :], load_sem.at[3]),
    ] + [
        pltpu.make_async_copy(q.at[0, :, pl.ds(u * UCOLS, UCOLS)], qbuf.at[u], load_sem.at[4 + u])
        for u in range(units)
    ]
    for copy in loads:
        copy.start()

    barrier = pltpu.get_barrier_semaphore()
    for peer in (other, zp, fwd, bwd):
        pl.semaphore_signal(barrier, inc=1, device_id=peer, device_id_type=MESH)
    pl.semaphore_wait(barrier, 4)

    def remote(src, dst, send, recv, to):
        return pltpu.make_async_remote_copy(
            src_ref=src, dst_ref=dst, send_sem=send, recv_sem=recv, device_id=to, device_id_type=MESH
        )

    def kv_copies():
        return [
            remote(ck.at[0], ckb.at[pl.ds(ROWS, ROWS), :], kv_send.at[2], kv_recv.at[2], other),
            remote(pk, kall.at[:, pl.ds(kd, kd), :], kv_send.at[0], kv_recv.at[0], other),
            remote(pv, vall.at[:, pl.ds(kd, kd), :], kv_send.at[1], kv_recv.at[1], other),
            remote(cv.at[0], cvb.at[pl.ds(ROWS, ROWS), :], kv_send.at[3], kv_recv.at[3], other),
        ]

    def q_copy(number, u, place_from, place_to, to):
        src = q.at[0, :, pl.ds(u * UCOLS, UCOLS)] if place_from is None else qbuf.at[place_from * units + u]
        k = place_to * units + u
        return remote(src, qbuf.at[k], q_send.at[number * units + u], q_recv.at[k], to)

    sends0 = []
    for u in range(units):
        sends0 += [
            q_copy(0, u, None, T1, fwd),
            q_copy(1, u, None, T2, bwd),
            q_copy(2, u, None, T3, zp),
        ]
    kvs = kv_copies()
    for copy in sends0[:3]:
        copy.start()
    for copy in kvs:
        copy.start()
    for copy in sends0[3:]:
        copy.start()

    mine, theirs = tiles[me], tiles[me + d]
    for place, (zf, steps) in enumerate(PLACES):
        tile = tiles[seq(zf, steps)]
        info[place, 0] = prompts[tile // 4]
        for k, held in enumerate((mine, theirs)):
            gap = (tile % 2 - held % 2) * ROWS
            info[place, 1 + k] = jnp.where(tile // 2 == held // 2, gap, -4 * ROWS)

    ahead = lax.broadcasted_iota(jnp.int32, (UROWS, ROWS), 1) - (
        lax.broadcasted_iota(jnp.int32, (UROWS, ROWS), 0) % ROWS
    )

    def wait_in(buf, sems, k):
        pltpu.make_async_copy(buf.at[k], buf.at[k], sems.at[k]).wait()

    def o_copy(number, u, place, slot, to):
        k, j = place * units + u, slot * units + u
        return (
            remote(obuf.at[k], rbuf.at[j], o_send.at[number * units + u], o_recv.at[j], to),
            remote(lob.at[k], lrb.at[j], l_send.at[number * units + u], l_recv.at[j], to),
        )

    def send_out(number, u, place, slot, to):
        for copy in o_copy(number, u, place, slot, to):
            copy.start()

    def merged(u, place, slots):
        k = place * units + u
        js = [slot * units + u for slot in slots]
        for j in js:
            wait_in(rbuf, o_recv, j)
            wait_in(lrb, l_recv, j)
        logs = [lob[k]] + [lrb[j] for j in js]
        peak = functools.reduce(jnp.maximum, logs)
        weights = [jnp.exp2(x - peak) for x in logs]
        total = functools.reduce(jnp.add, weights)
        values = [obuf[k]] + [rbuf[j] for j in js]
        parts = []
        for head in range(HEADS_UNIT):
            acc = None
            for w, v in zip(weights, values):
                share = (w / total)[head : head + 1, :]
                column = jnp.broadcast_to(share, (ROWS, ROWS)).T
                term = column * v[:, head * WIDTH : (head + 1) * WIDTH].astype(jnp.float32)
                acc = term if acc is None else acc + term
            parts.append(acc)
        return jnp.concatenate(parts, axis=1), peak + jnp.log2(total)

    def merge_send(number, u, place, slots, slot, to):
        o, log = merged(u, place, slots)
        obuf[place * units + u] = o.astype(jnp.bfloat16)
        lob[place * units + u] = log
        send_out(number, u, place, slot, to)

    def q_ready(n):
        @pl.when(n >= units)
        def _():
            wait_in(qbuf, q_recv, n)

    def relay1(u):
        wait_in(qbuf, q_recv, T1 * units + u)
        q_copy(3, u, T1, T6, fwd).start()
        wait_in(qbuf, q_recv, T3 * units + u)
        q_copy(4, u, T3, T4, fwd).start()
        q_copy(5, u, T3, T5, bwd).start()

    def relay2(u):
        wait_in(qbuf, q_recv, T6 * units + u)
        q_copy(6, u, T6, T7, zp).start()

    waited_by_relay = (T1, T3, T6)

    def before(n):
        @pl.when((n < 2 * units) & (n % 2 == 1))
        def _():
            relay1(n // 2)

        @pl.when((n >= 2 * units) & (n < 4 * units) & (n % 2 == 0))
        def _():
            relay2((n - 2 * units) // 2)

        place = n // units

        @pl.when((place == T2) | (place == T5) | (place == T7) | (place == T4))
        def _():
            wait_in(qbuf, q_recv, n)

    def after(n):
        place, u = n // units, n % units

        @pl.when(place == T2)
        def _():
            send_out(0, u, T2, IN02, fwd)

        @pl.when(place == T5)
        def _():
            send_out(1, u, T5, IN35, fwd)

        @pl.when(place == T7)
        def _():
            send_out(2, u, T7, IN67, zp)

        @pl.when(place == T4)
        def _():
            send_out(3, u, T4, IN34, bwd)

        @pl.when(place == T6)
        def _():
            merge_send(4, u, T6, (IN67,), IN16, bwd)

        @pl.when(place == T3)
        def _():
            merge_send(5, u, T3, (IN34, IN35), IN03, zp)

    chunks = [(i * CHUNK, CHUNK) for i in range(2 * kd // CHUNK)]
    total_keys = 2 * kd

    def fold(op, x):
        parts = [x[:, i : i + 128] for i in range(0, x.shape[1], 128)]
        return functools.reduce(op, parts)

    def both(n1, s1, m1, n2, s2, m2):
        first = n1 is not None
        second = n2 is not None
        if first:
            place1 = n1 // units
            p1 = info[place1, 0]
            raw = qbuf[n1]
            query = jnp.concatenate([raw[:, i * WIDTH : (i + 1) * WIDTH] for i in range(HEADS_UNIT)], axis=0)
            peak = None
        if second:
            p2 = info[n2 // units, 0]
            low = m2[...]
            sums = jnp.zeros((UROWS, 128), jnp.float32)
            acc = jnp.zeros((UROWS, WIDTH), jnp.float32)
        for at, size in chunks + [(total_keys, 2 * ROWS)]:
            own = at >= total_keys
            if first:
                keys = ckb[...] if own else kall[p1, pl.ds(at, size), :]
                s = across(query, keys)
                if own:
                    s = jnp.concatenate(
                        [
                            jnp.where(ahead <= info[place1, 1 + k], s[:, k * ROWS : (k + 1) * ROWS], VERY_LOW)
                            for k in range(2)
                        ],
                        axis=1,
                    )
                s1[:, pl.ds(at, size)] = s
                top = fold(jnp.maximum, s)
                peak = top if peak is None else jnp.maximum(peak, top)
            if second:
                rows = cvb[...] if own else vall[p2, pl.ds(at, size), :]
                w = jnp.exp2(s2[:, pl.ds(at, size)] * SCALE - jnp.concatenate([low] * (size // 128), axis=1))
                sums = sums + fold(jnp.add, w)
                acc = acc + jnp.dot(w.astype(jnp.bfloat16), rows, preferred_element_type=jnp.float32)
        if first:
            m1[...] = jnp.broadcast_to(jnp.max(peak, axis=1, keepdims=True) * SCALE, (UROWS, 128))
        if second:
            total = jnp.sum(sums, axis=1, keepdims=True)
            o = acc / total
            for i in range(HEADS_UNIT):
                obuf[n2, :, i * WIDTH : (i + 1) * WIDTH] = o[i * ROWS : (i + 1) * ROWS].astype(jnp.bfloat16)
            log = low + jnp.log2(total)
            for i in range(HEADS_UNIT):
                lob[n2, i : i + 1, :] = log[i * ROWS : (i + 1) * ROWS].T[0:1, :]

    lob[...] = jnp.zeros_like(lob)
    for copy in loads:
        copy.wait()
    for copy in kvs:
        copy.wait_recv()
    both(0, sa, ma, None, None, None)

    last = 8 * units - 1

    def step(k, carry):
        n = 2 * k
        before(n + 1)
        both(n + 1, sb, mb, n, sa, ma)
        after(n)
        before(jnp.minimum(n + 2, last + 1))
        both(jnp.minimum(n + 2, last), sa, ma, n + 1, sb, mb)
        after(n + 1)
        return carry

    lax.fori_loop(0, 4 * units, step, 0)

    for u in range(units):
        merge_send(6, u, T1, (IN16,), IN01, bwd)

    tile = tiles[me]
    limit = lengths[tile // 4, tile // 2 % 2] - tile % 2 * ROWS
    live = lax.broadcasted_iota(jnp.int32, (ROWS, UCOLS), 0) < limit
    for u in range(units):
        o, _ = merged(u, T0, (IN02, IN03, IN01))
        out[0, :, u * UCOLS : (u + 1) * UCOLS] = jnp.where(live, o, 0.0).astype(jnp.bfloat16)

    for copy in sends0 + kvs:
        copy.wait_send()

    def drain(u, carry):
        for number, src, dst, to in ((3, T1, T6, fwd), (4, T3, T4, fwd), (5, T3, T5, bwd), (6, T6, T7, zp)):
            q_copy(number, u, src, dst, to).wait_send()
        for number, place, slot, to in (
            (0, T2, IN02, fwd), (1, T5, IN35, fwd), (2, T7, IN67, zp), (3, T4, IN34, bwd),
            (4, T6, IN16, bwd), (5, T3, IN03, zp), (6, T1, IN01, bwd),
        ):
            for copy in o_copy(number, u, place, slot, to):
                copy.wait_send()
        return carry

    lax.fori_loop(0, units, drain, 0)


def attend(lengths, prompts, tiles, q, ck, cv, pk, pv):
    units = q.shape[2] // UCOLS
    kd = pk.shape[1]
    keys = 2 * kd + 2 * ROWS
    bf, f32 = jnp.bfloat16, jnp.float32
    smem = pl.BlockSpec(memory_space=pltpu.SMEM)
    hbm = pl.BlockSpec(memory_space=pl.ANY)
    dma = pltpu.SemaphoreType.DMA
    return pl.pallas_call(
        functools.partial(attend_kernel, units),
        out_shape=jax.ShapeDtypeStruct(q.shape, bf),
        in_specs=[smem] * 3 + [hbm] * 5,
        out_specs=pl.BlockSpec(memory_space=pltpu.VMEM),
        scratch_shapes=[
            pltpu.VMEM((2, 2 * kd, WIDTH), bf),
            pltpu.VMEM((2, 2 * kd, WIDTH), bf),
            pltpu.VMEM((2 * ROWS, WIDTH), bf),
            pltpu.VMEM((2 * ROWS, WIDTH), bf),
            pltpu.VMEM((8 * units, ROWS, UCOLS), bf),
            pltpu.VMEM((8 * units, ROWS, UCOLS), bf),
            pltpu.VMEM((7 * units, ROWS, UCOLS), bf),
            pltpu.VMEM((8 * units, 8, ROWS), f32),
            pltpu.VMEM((7 * units, 8, ROWS), f32),
            pltpu.VMEM((UROWS, keys), f32),
            pltpu.VMEM((UROWS, keys), f32),
            pltpu.VMEM((UROWS, 128), f32),
            pltpu.VMEM((UROWS, 128), f32),
            pltpu.SMEM((8, 4), jnp.int32),
            dma((4 + units,)),
            dma((4,)),
            dma((4,)),
            dma((7 * units,)),
            dma((8 * units,)),
            dma((7 * units,)),
            dma((7 * units,)),
            dma((7 * units,)),
            dma((7 * units,)),
        ],
        compiler_params=pltpu.CompilerParams(
            collective_id=0, has_side_effects=True, vmem_limit_bytes=48 << 20
        ),
        name="attend",
    )(lengths, prompts, tiles, q, ck, cv, pk, pv)


def split_up(x, dim, length):
    before, after = (x.shape[:dim], x.shape[dim + 1 :])
    return jnp.moveaxis(x.reshape(*before, length, -1, *after), dim, 0)


def summed_on_arrival(x, axis, dim):
    length = lax.axis_size(axis)
    blocks = lax.all_to_all(split_up(x, dim, length), axis, 0, 0, tiled=True)
    return jnp.sum(blocks.astype(jnp.float32), axis=0)


def local(q, ck, cv, pk, pv, lengths, prompts, tiles, weight):
    attention = attend(lengths, prompts, tiles, q, ck, cv, pk, pv)
    partial_out = jnp.einsum(
        "stc,cd->std",
        lax.all_gather(attention, "seq", axis=0, tiled=True),
        weight,
        preferred_element_type=jnp.float32,
    )
    return summed_on_arrival(partial_out.astype(jnp.bfloat16), "head", 0).astype(jnp.bfloat16)


def solution(mesh):
    return jax.shard_map(
        local,
        mesh=mesh,
        in_specs=(
            P("seq", None, "head"),
            P("seq", None, "head"),
            P("seq", None, "head"),
            P(None, "seq", "head"),
            P(None, "seq", "head"),
            P(),
            P(),
            P(),
            P("head", "seq"),
        ),
        out_specs=P("head", None, "seq"),
        check_vma=False,
    )
```

time: 312 us -> 151 us (0.48)
  waiting for transfers between devices: 165 us -> 39.1 us
  matrix products: 63.7 us -> 4.53 us
  Pallas kernels: 0 us -> 49.4 us
  other arithmetic: 16.3 us -> 1.05 us
  between operations: 17.8 us -> 13.4 us
  local copies, waits for them, and re-layouts: 10.5 us -> 6.71 us
    all_gather x3 -> x0, waiting for transfers between devices: 126 us -> none  [the longest x1 54.6 us: local(): lax.all_gather(cached_prompt_values, 'seq', axis=1, tiled=True)]
    dot_general x34 -> x0, matrix products: 59.2 us -> none  [the longest x17 32 us: weigh_values(): jnp.einsum('kgtp,pkd->kgtd', weights.astype(jnp.bfloat16), value_rows, pr...]
    pallas_call x0 -> x1, Pallas kernels: none -> 49.4 us  [attend(): pl.pallas_call(functools.partial(attend_kernel, units), out_shape=jax.Sha...]
    reduce_sum x17 -> x0, other arithmetic: 11.2 us -> none  [the longest x16 11 us: one_block(): total_new = totals_in[0] * keep + jnp.sum(weights, axis=3)]
    unnamed x6 -> x17, local copies, waits for them, and re-layouts: 1.77 us -> 6.71 us
  transfers between devices with their start and end apart: 4 -> 1, of which waited for: 4 -> 1; matrix products, arithmetic and copies ran while one was open for 4% -> 0% of each run, Pallas kernels for 0% -> 0%
where the time goes in v1:
time: 151 us; the launch traced here: 148 us
  Pallas kernels  49.4 us (33%)
  waiting for transfers between devices  39.1 us (26%)
  blocking collectives  34.4 us (23%)
  between operations  13.4 us (9%)
  local copies, waits for them, and re-layouts  6.71 us (4%)
  matrix products  4.53 us (3%)
    pallas_call x1, Pallas kernels, attend(): pl.pallas_call(functools.partial(attend_kernel, units), out_shape=jax.Sha...  49.4 us
    all_gather x1, waiting for transfers between devices, local(): lax.all_gather(attention, 'seq', axis=0, tiled=True)  39 us
    all_to_all x1, blocking collectives, summed_on_arrival(): blocks = lax.all_to_all(split_up(x, dim, length), axis, 0, 0, tiled=True)  34.4 us
    unnamed x17, local copies, waits for them, and re-layouts  6.71 us
    dot_general x1, matrix products, local(): jnp.einsum('stc,cd->std', lax.all_gather(attention, 'seq', axis=0, tiled=...  4.53 us
  transfers between devices with their start and end apart: 1, of which 1 were waited for; matrix products, arithmetic and copies ran while one was open for 0% of the time, Pallas kernels for 0%

profile of v1, /device:TPU:48, one launch (start us, length us, event | category | flops | bytes accessed | tf_op | source)
XLA Modules:
  0.0 148.5 jit_solution(12104412947263756748)
XLA Ops:
  6.5 0.0 copy-start
  6.5 0.0 all-gather.2.cloned.1.call-start
  6.5 0.9 copy.11.lengths
  7.4 0.0 copy-start.1
  7.4 1.0 copy-done.1
  8.4 0.0 copy-start.2
  8.4 1.0 copy-done.2
  9.5 0.0 copy-start.3
  9.5 0.9 copy-done.3
  10.4 0.0 copy-start.4
  10.4 0.8 copy-done.4
  11.2 0.0 copy-start.5
  11.2 0.8 copy-done.5
  11.9 0.0 copy-start.6
  11.9 0.7 copy-done.6
  12.6 0.0 copy-start.7
  12.6 0.7 copy-done.7
  13.3 49.4 %attend.1 = bf16[1,128,1024]{2,1,0:T(8,128)(2,1)} custom-call(s32[4,2]{1,0:T(4,128)S(1)} %copy.11.lengths, s32[4]{0:T(128)S(1)} %copy-done.6, s32[16]{0:T(128)S(1)} %copy-done.7, bf16[1,128,1024]{2,1,0:T(8,128)(2,1)S(1)} %copy-done.3, bf16[1,128,128]{2,1,0:T(8,128)(2,1)S(1)} %copy-done.4, bf16[1,128,128]{2,1,0:T(8,128)(2,1)S(1)} %copy-done.5, ...), custom_call_target="tpu_custom_call" | custom-call | tf_op jit(solution)/shard_map/attend/pallas_call | solution.py:327
  62.6 0.0 all-gather.2.cloned.1.call-update
  62.6 39.0 %all-gather.2.cloned.1.call-done = bf16[16,128,1024]{2,1,0:T(8,128)(2,1)} async-done(((bf16[1,128,1024]{2,1,0:T(8,128)(2,1)}), bf16[16,128,1024]{2,1,0:T(8,128)(2,1)}) %all-gather.2.cloned.1.call-update) | async-done | bytes 4194320 | tf_op jit(solution)/shard_map/all_gather | solution.py:379
  101.7 0.0 copy-done
  101.7 4.5 %convolution_convert_fusion = bf16[16,128,512]{2,1,0:T(8,128)(2,1)S(1)} fusion(bf16[16,128,1024]{2,1,0:T(8,128)(2,1)} %all-gather.2.cloned.1.call-done, bf16[1024,512]{1,0:T(8,128)(2,1)S(1)} %copy-done), kind=kOutput, calls=%fused_computation | convolution fusion | flops 2148532224 | bytes 7340032 | tf_op jit(solution)/shard_map/stc,cd->std/dot_general | solution.py:377
  106.2 34.4 %all_to_all.5 = bf16[8,2,128,512]{3,2,1,0:T(8,128)(2,1)S(1)} all-to-all(bf16[8,2,128,512]{3,2,1,0:T(8,128)(2,1)S(1)} %bitcast.5), channel_id=1, replica_groups=mesh['seq'=16,'head'=8] {'head'}, dimensions={0} | all-to-all | bytes 4194304 | tf_op jit(solution)/shard_map/all_to_all | solution.py:371
  140.6 1.0 reduce_sum.12
Async XLA Ops:
  6.5 95.2 %copy-start = (bf16[1024,512]{1,0:T(8,128)(2,1)S(1)}, bf16[1024,512]{1,0:T(8,128)(2,1)}, u32[]{:S(2)}) copy-start(bf16[1024,512]{1,0:T(8,128)(2,1)} %param.17) | copy-start | bytes 3145732
  6.5 95.2 %all-gather.2.cloned.1.call-start = ((), (), s32[]{:S(2)}) async-start(), calls=%async_computation.1 | async-start | bytes 4456448 | tf_op jit(solution)/shard_map/all_gather | solution.py:379
  7.4 1.0 copy-start.1
  8.4 1.0 copy-start.2
  9.5 0.9 copy-start.3
  10.4 0.8 copy-start.4
  11.2 0.8 copy-start.5
  11.9 0.7 copy-start.6
  12.6 0.7 copy-start.7
Sparse Core Ops, SparseCore 0:
  62.8 38.8 all-gather.1

commit v2 on v1

--- a/solution.py
+++ b/solution.py
@@ -32,10 +32,12 @@
 
 def attend_kernel(
     units,
-    lengths, prompts, tiles, q, ck, cv, pk, pv,
+    lengths, prompts, tiles, q, ck, cv, pk, pv, weight,
     out,
     kall, vall, ckb, cvb, qbuf, obuf, rbuf, lob, lrb, sa, sb, ma, mb, info,
+    wbuf, abuf, pbuf, far_in, leaf_in, inter_in, zin, zout, fin, xout,
     load_sem, kv_send, kv_recv, q_send, q_recv, o_send, o_recv, l_send, l_recv,
+    a_send, a_recv, far_send, far_recv, leaf_send, leaf_recv, inter_send, inter_recv, z_send, z_recv, x_sem,
 ):
     me = lax.axis_index("seq")
     z, y, c = me // 8, (me // 2) % 4, me % 2
@@ -50,6 +52,11 @@
 
     other = {"seq": me + d}
     zp, fwd, bwd = dev(1, 0), dev(0, 1), dev(0, -1)
+    group = lax.axis_index("head")
+    x, zh = group // 2, group % 2
+    xfwd = {"head": (x + d + 4) % 4 * 2 + zh}
+    xbwd = {"head": (x - d + 4) % 4 * 2 + zh}
+    zhp = {"head": x * 2 + 1 - zh}
 
     loads = [
         pltpu.make_async_copy(pk, kall.at[:, pl.ds(0, kd), :], load_sem.at[0]),
@@ -60,13 +67,14 @@
         pltpu.make_async_copy(q.at[0, :, pl.ds(u * UCOLS, UCOLS)], qbuf.at[u], load_sem.at[4 + u])
         for u in range(units)
     ]
+    wload = pltpu.make_async_copy(weight, wbuf.at[c], load_sem.at[4 + units])
     for copy in loads:
         copy.start()
 
     barrier = pltpu.get_barrier_semaphore()
-    for peer in (other, zp, fwd, bwd):
+    for peer in (other, zp, fwd, bwd, xfwd, xbwd, zhp):
         pl.semaphore_signal(barrier, inc=1, device_id=peer, device_id_type=MESH)
-    pl.semaphore_wait(barrier, 4)
+    pl.semaphore_wait(barrier, 7)
 
     def remote(src, dst, send, recv, to):
         return pltpu.make_async_remote_copy(
@@ -80,6 +88,8 @@
             remote(pv, vall.at[:, pl.ds(kd, kd), :], kv_send.at[1], kv_recv.at[1], other),
             remote(cv.at[0], cvb.at[pl.ds(ROWS, ROWS), :], kv_send.at[3], kv_recv.at[3], other),
         ]
+
+    wsend = remote(weight, wbuf.at[c], kv_send.at[4], kv_recv.at[4], other)
 
     def q_copy(number, u, place_from, place_to, to):
         src = q.at[0, :, pl.ds(u * UCOLS, UCOLS)] if place_from is None else qbuf.at[place_from * units + u]
@@ -100,6 +110,8 @@
         copy.start()
     for copy in sends0[3:]:
         copy.start()
+    wload.start()
+    wsend.start()
 
     mine, theirs = tiles[me], tiles[me + d]
     for place, (zf, steps) in enumerate(PLACES):
@@ -292,19 +304,135 @@
     for u in range(units):
         merge_send(6, u, T1, (IN16,), IN01, bwd)
 
+    def a_copy(number, u, place_from, place_to, to):
+        k = place_to * units + u
+        return remote(
+            abuf.at[place_from * units + u], abuf.at[k], a_send.at[number * units + u], a_recv.at[k], to
+        )
+
+    def a_relay1(u):
+        wait_in(abuf, a_recv, T1 * units + u)
+        a_copy(3, u, T1, T6, fwd).start()
+        wait_in(abuf, a_recv, T3 * units + u)
+        a_copy(4, u, T3, T4, fwd).start()
+        a_copy(5, u, T3, T5, bwd).start()
+
+    def a_relay2(u):
+        wait_in(abuf, a_recv, T6 * units + u)
+        a_copy(6, u, T6, T7, zp).start()
+
     tile = tiles[me]
     limit = lengths[tile // 4, tile // 2 % 2] - tile % 2 * ROWS
     live = lax.broadcasted_iota(jnp.int32, (ROWS, UCOLS), 0) < limit
     for u in range(units):
         o, _ = merged(u, T0, (IN02, IN03, IN01))
-        out[0, :, u * UCOLS : (u + 1) * UCOLS] = jnp.where(live, o, 0.0).astype(jnp.bfloat16)
-
-    for copy in sends0 + kvs:
+        abuf[T0 * units + u] = jnp.where(live, o, 0.0).astype(jnp.bfloat16)
+        a_copy(0, u, T0, T1, fwd).start()
+        a_copy(1, u, T0, T2, bwd).start()
+        a_copy(2, u, T0, T3, zp).start()
+
+    def far_copy(zt, part, source):
+        k = zt * 2 + part
+        return remote(pbuf.at[source * 2 + part], far_in.at[k], far_send.at[k], far_recv.at[k], xbwd)
+
+    def leaf_copy(zt, part, source):
+        k = zt * 2 + part
+        return remote(pbuf.at[source * 2 + part], leaf_in.at[k], leaf_send.at[k], leaf_recv.at[k], xfwd)
+
+    def inter_copy(zt, part, source):
+        k = zt * 2 + part
+        return remote(pbuf.at[source * 2 + part], inter_in.at[k], inter_send.at[k], inter_recv.at[k], xbwd)
+
+    def project(place):
+        zf, steps = PLACES[place]
+        home = seq(zf, steps) // 2
+        rows = jnp.concatenate([abuf[place * units + u] for u in range(units)], axis=1)
+        for part in range(2):
+            pbuf[home * 2 + part] = jnp.dot(rows, wbuf[part], preferred_element_type=jnp.float32).astype(
+                jnp.bfloat16
+            )
+        gap = (home // 2 - x + 4) % 4
+
+        @pl.when(gap == 2)
+        def _():
+            for part in range(2):
+                far_copy(home % 2, part, home).start()
+
+        @pl.when(gap == (d + 4) % 4)
+        def _():
+            for part in range(2):
+                leaf_copy(home % 2, part, home).start()
+
+    def settle(place):
+        for u in range(units):
+            wait_in(abuf, a_recv, place * units + u)
+
+    wload.wait()
+    wsend.wait_recv()
+    project(T0)
+    for u in range(units):
+        a_relay1(u)
+    project(T1)
+    project(T3)
+    settle(T2)
+    project(T2)
+    for u in range(units):
+        a_relay2(u)
+    project(T6)
+    settle(T5)
+    project(T5)
+    settle(T4)
+    project(T4)
+    settle(T7)
+    project(T7)
+
+    f32 = jnp.float32
+    inter_home = (x - d + 4) % 4 * 2
+    for zt in (1 - zh, zh):
+        for part in range(2):
+            k, m = zt * 2 + part, (inter_home + zt) * 2 + part
+            wait_in(far_in, far_recv, k)
+            pbuf[m] = (pbuf[m].astype(f32) + far_in[k].astype(f32)).astype(jnp.bfloat16)
+            inter_copy(zt, part, inter_home + zt).start()
+
+    def column_sum(zt, part):
+        k = zt * 2 + part
+        wait_in(leaf_in, leaf_recv, k)
+        wait_in(inter_in, inter_recv, k)
+        here = pbuf[(x * 2 + zt) * 2 + part].astype(f32)
+        return here + leaf_in[k].astype(f32) + inter_in[k].astype(f32)
+
+    def z_copy(part):
+        return remote(zout.at[part], zin.at[part], z_send.at[part], z_recv.at[part], zhp)
+
+    for part in range(2):
+        zout[part] = column_sum(1 - zh, part).astype(jnp.bfloat16)
+        z_copy(part).start()
+    for part in range(2):
+        fin[part] = column_sum(zh, part)
+    for part in range(2):
+        wait_in(zin, z_recv, part)
+    xout[...] = (fin[1 - c] + zin[1 - c].astype(f32)).astype(jnp.bfloat16)
+    last_copy = remote(xout, out.at[c], x_sem.at[0], x_sem.at[1], other)
+    last_copy.start()
+    out[c] = (fin[c] + zin[c].astype(f32)).astype(jnp.bfloat16)
+    last_copy.wait()
+
+    for copy in sends0 + kvs + [wsend]:
         copy.wait_send()
+    for part in range(2):
+        z_copy(part).wait_send()
+        for zt in range(2):
+            far_copy(zt, part, 0).wait_send()
+            leaf_copy(zt, part, 0).wait_send()
+            inter_copy(zt, part, 0).wait_send()
 
     def drain(u, carry):
-        for number, src, dst, to in ((3, T1, T6, fwd), (4, T3, T4, fwd), (5, T3, T5, bwd), (6, T6, T7, zp)):
-            q_copy(number, u, src, dst, to).wait_send()
+        for make in (q_copy, a_copy):
+            for number, src, dst, to in ((3, T1, T6, fwd), (4, T3, T4, fwd), (5, T3, T5, bwd), (6, T6, T7, zp)):
+                make(number, u, src, dst, to).wait_send()
+        for number, dst, to in ((0, T1, fwd), (1, T2, bwd), (2, T3, zp)):
+            a_copy(number, u, T0, dst, to).wait_send()
         for number, place, slot, to in (
             (0, T2, IN02, fwd), (1, T5, IN35, fwd), (2, T7, IN67, zp), (3, T4, IN34, bwd),
             (4, T6, IN16, bwd), (5, T3, IN03, zp), (6, T1, IN01, bwd),
@@ -316,9 +444,10 @@
     lax.fori_loop(0, units, drain, 0)
 
 
-def attend(lengths, prompts, tiles, q, ck, cv, pk, pv):
+def attend(lengths, prompts, tiles, q, ck, cv, pk, pv, weight):
     units = q.shape[2] // UCOLS
     kd = pk.shape[1]
+    cols = weight.shape[1]
     keys = 2 * kd + 2 * ROWS
     bf, f32 = jnp.bfloat16, jnp.float32
     smem = pl.BlockSpec(memory_space=pltpu.SMEM)
@@ -326,8 +455,8 @@
     dma = pltpu.SemaphoreType.DMA
     return pl.pallas_call(
         functools.partial(attend_kernel, units),
-        out_shape=jax.ShapeDtypeStruct(q.shape, bf),
-        in_specs=[smem] * 3 + [hbm] * 5,
+        out_shape=jax.ShapeDtypeStruct((2, ROWS, weight.shape[1]), bf),
+        in_specs=[smem] * 3 + [hbm] * 6,
         out_specs=pl.BlockSpec(memory_space=pltpu.VMEM),
         scratch_shapes=[
             pltpu.VMEM((2, 2 * kd, WIDTH), bf),
@@ -344,43 +473,46 @@
             pltpu.VMEM((UROWS, 128), f32),
             pltpu.VMEM((UROWS, 128), f32),
             pltpu.SMEM((8, 4), jnp.int32),
-            dma((4 + units,)),
-            dma((4,)),
-            dma((4,)),
+            pltpu.VMEM((2,) + weight.shape, bf),
+            pltpu.VMEM((8 * units, ROWS, UCOLS), bf),
+            pltpu.VMEM((16, ROWS, cols), bf),
+            pltpu.VMEM((4, ROWS, cols), bf),
+            pltpu.VMEM((4, ROWS, cols), bf),
+            pltpu.VMEM((4, ROWS, cols), bf),
+            pltpu.VMEM((2, ROWS, cols), bf),
+            pltpu.VMEM((2, ROWS, cols), bf),
+            pltpu.VMEM((2, ROWS, cols), f32),
+            pltpu.VMEM((ROWS, cols), bf),
+            dma((5 + units,)),
+            dma((5,)),
+            dma((5,)),
             dma((7 * units,)),
             dma((8 * units,)),
             dma((7 * units,)),
             dma((7 * units,)),
             dma((7 * units,)),
             dma((7 * units,)),
+            dma((7 * units,)),
+            dma((8 * units,)),
+            dma((4,)),
+            dma((4,)),
+            dma((4,)),
+            dma((4,)),
+            dma((4,)),
+            dma((4,)),
+            dma((2,)),
+            dma((2,)),
+            dma((2,)),
         ],
         compiler_params=pltpu.CompilerParams(
-            collective_id=0, has_side_effects=True, vmem_limit_bytes=48 << 20
+            collective_id=0, has_side_effects=True, vmem_limit_bytes=60 << 20
         ),
         name="attend",
-    )(lengths, prompts, tiles, q, ck, cv, pk, pv)
-
-
-def split_up(x, dim, length):
-    before, after = (x.shape[:dim], x.shape[dim + 1 :])
-    return jnp.moveaxis(x.reshape(*before, length, -1, *after), dim, 0)
-
-
-def summed_on_arrival(x, axis, dim):
-    length = lax.axis_size(axis)
-    blocks = lax.all_to_all(split_up(x, dim, length), axis, 0, 0, tiled=True)
-    return jnp.sum(blocks.astype(jnp.float32), axis=0)
+    )(lengths, prompts, tiles, q, ck, cv, pk, pv, weight)
 
 
 def local(q, ck, cv, pk, pv, lengths, prompts, tiles, weight):
-    attention = attend(lengths, prompts, tiles, q, ck, cv, pk, pv)
-    partial_out = jnp.einsum(
-        "stc,cd->std",
-        lax.all_gather(attention, "seq", axis=0, tiled=True),
-        weight,
-        preferred_element_type=jnp.float32,
-    )
-    return summed_on_arrival(partial_out.astype(jnp.bfloat16), "head", 0).astype(jnp.bfloat16)
+    return attend(lengths, prompts, tiles, q, ck, cv, pk, pv, weight)
 
 
 def solution(mesh):

time: 151 us -> 93.1 us (0.62)
  Pallas kernels: 49.4 us -> 88.6 us
  waiting for transfers between devices: 39.1 us -> 0 us
  blocking collectives: 34.4 us -> 0 us
  between operations: 13.4 us -> 0.01 us
  matrix products: 4.53 us -> 0 us
  local copies, waits for them, and re-layouts: 6.71 us -> 3.01 us
    pallas_call x1, Pallas kernels: 49.4 us -> 88.6 us  [attend(): pl.pallas_call(functools.partial(attend_kernel, units), out_shape=jax.Sha...]
    all_gather x1 -> x0, waiting for transfers between devices: 39 us -> none  [local(): lax.all_gather(attention, 'seq', axis=0, tiled=True)]
    all_to_all x1 -> x0, blocking collectives: 34.4 us -> none  [summed_on_arrival(): blocks = lax.all_to_all(split_up(x, dim, length), axis, 0, 0, tiled=True)]
    dot_general x1 -> x0, matrix products: 4.53 us -> none  [local(): jnp.einsum('stc,cd->std', lax.all_gather(attention, 'seq', axis=0, tiled=...]
    unnamed x17 -> x2, local copies, waits for them, and re-layouts: 6.71 us -> 3.01 us
  transfers between devices with their start and end apart: 1 -> 0, of which waited for: 1 -> 0; matrix products, arithmetic and copies ran while one was open for 0% -> 0% of each run, Pallas kernels for 0% -> 0%
where the time goes in v2:
time: 93.1 us; the launch traced here: 91.6 us
  Pallas kernels  88.6 us (95%)
  local copies, waits for them, and re-layouts  3.01 us (3%)
    pallas_call x1, Pallas kernels, attend(): pl.pallas_call(functools.partial(attend_kernel, units), out_shape=jax.Sha...  88.6 us
    unnamed x2, local copies, waits for them, and re-layouts  3.01 us

profile of v2, /device:TPU:48, one launch (start us, length us, event | category | flops | bytes accessed | tf_op | source)
XLA Modules:
  0.0 91.6 jit_solution(3543046044596115362)
XLA Ops:
  0.0 1.3 %copy.10.lengths = s32[4,2]{1,0:T(4,128)} copy(s32[4,2]{0,1:T(2,128)} %param.14) | data formatting | bytes 64 | tf_op args[5]
  1.3 88.6 %attend.1 = bf16[2,128,512]{2,1,0:T(8,128)(2,1)} custom-call(s32[4,2]{1,0:T(4,128)} %copy.10.lengths, s32[4]{0:T(128)} %prompts.1, s32[16]{0:T(128)} %tiles.1, bf16[1,128,1024]{2,1,0:T(8,128)(2,1)} %q.1, bf16[1,128,128]{2,1,0:T(8,128)(2,1)} %ck.1, bf16[1,128,128]{2,1,0:T(8,128)(2,1)} %cv.1, bf16[2,1024,128]{2,1,0:T(8,128)(2,1)} %pk.1, ...), custom_call_target="tpu_custom_call" | custom-call | tf_op jit(solution)/shard_map/attend/pallas_call | solution.py:456
  89.9 1.7 %copy.12 = bf16[2,128,512]{2,1,0:T(8,128)(2,1)} copy(bf16[2,128,512]{2,1,0:T(8,128)(2,1)} %attend.1) | data formatting | bytes 524288

commit v3 on v2

--- a/solution.py
+++ b/solution.py
@@ -34,7 +34,7 @@
     units,
     lengths, prompts, tiles, q, ck, cv, pk, pv, weight,
     out,
-    kall, vall, ckb, cvb, qbuf, obuf, rbuf, lob, lrb, sa, sb, ma, mb, info,
+    kall, vall, ckb, cvb, qbuf, obuf, rbuf, lob, lrb, sa, sb, ma, mb, low_a, low_b, sums_a, sums_b, acc_a, acc_b, info,
     wbuf, abuf, pbuf, far_in, leaf_in, inter_in, zin, zout, fin, xout,
     load_sem, kv_send, kv_recv, q_send, q_recv, o_send, o_recv, l_send, l_recv,
     a_send, a_recv, far_send, far_recv, leaf_send, leaf_recv, inter_send, inter_recv, z_send, z_recv, x_sem,
@@ -167,11 +167,6 @@
         lob[place * units + u] = log
         send_out(number, u, place, slot, to)
 
-    def q_ready(n):
-        @pl.when(n >= units)
-        def _():
-            wait_in(qbuf, q_recv, n)
-
     def relay1(u):
         wait_in(qbuf, q_recv, T1 * units + u)
         q_copy(3, u, T1, T6, fwd).start()
@@ -183,22 +178,22 @@
         wait_in(qbuf, q_recv, T6 * units + u)
         q_copy(6, u, T6, T7, zp).start()
 
-    waited_by_relay = (T1, T3, T6)
-
-    def before(n):
-        @pl.when((n < 2 * units) & (n % 2 == 1))
-        def _():
-            relay1(n // 2)
-
-        @pl.when((n >= 2 * units) & (n < 4 * units) & (n % 2 == 0))
-        def _():
-            relay2((n - 2 * units) // 2)
-
-        place = n // units
-
-        @pl.when((place == T2) | (place == T5) | (place == T7) | (place == T4))
-        def _():
-            wait_in(qbuf, q_recv, n)
+    def before(k):
+        @pl.when(k < units)
+        def _():
+            relay1(k)
+
+        @pl.when((k >= units) & (k < 2 * units))
+        def _():
+            relay2(k - units)
+
+        for ahead_by in (1, 2):
+            n = 2 * k + ahead_by
+            place = n // units
+
+            @pl.when((place == T2) | (place == T5) | (place == T7) | (place == T4))
+            def _():
+                wait_in(qbuf, q_recv, n)
 
     def after(n):
         place, u = n // units, n % units
@@ -234,7 +229,7 @@
         parts = [x[:, i : i + 128] for i in range(0, x.shape[1], 128)]
         return functools.reduce(op, parts)
 
-    def both(n1, s1, m1, n2, s2, m2):
+    def both(n1, s1, m1, n2, s2, m2, low2, sums2, acc2):
         first = n1 is not None
         second = n2 is not None
         if first:
@@ -245,7 +240,7 @@
             peak = None
         if second:
             p2 = info[n2 // units, 0]
-            low = m2[...]
+            low = jnp.broadcast_to(jnp.max(m2[...], axis=1, keepdims=True) * SCALE, (UROWS, 128))
             sums = jnp.zeros((UROWS, 128), jnp.float32)
             acc = jnp.zeros((UROWS, WIDTH), jnp.float32)
         for at, size in chunks + [(total_keys, 2 * ROWS)]:
@@ -270,36 +265,44 @@
                 sums = sums + fold(jnp.add, w)
                 acc = acc + jnp.dot(w.astype(jnp.bfloat16), rows, preferred_element_type=jnp.float32)
         if first:
-            m1[...] = jnp.broadcast_to(jnp.max(peak, axis=1, keepdims=True) * SCALE, (UROWS, 128))
+            m1[...] = peak
         if second:
-            total = jnp.sum(sums, axis=1, keepdims=True)
-            o = acc / total
-            for i in range(HEADS_UNIT):
-                obuf[n2, :, i * WIDTH : (i + 1) * WIDTH] = o[i * ROWS : (i + 1) * ROWS].astype(jnp.bfloat16)
-            log = low + jnp.log2(total)
-            for i in range(HEADS_UNIT):
-                lob[n2, i : i + 1, :] = log[i * ROWS : (i + 1) * ROWS].T[0:1, :]
+            low2[...] = low
+            sums2[...] = sums
+            acc2[...] = acc
+
+    def finish(n, low2, sums2, acc2):
+        total = jnp.sum(sums2[...], axis=1, keepdims=True)
+        o = acc2[...] / total
+        log = low2[...] + jnp.log2(total)
+        for i in range(HEADS_UNIT):
+            obuf[n, :, i * WIDTH : (i + 1) * WIDTH] = o[i * ROWS : (i + 1) * ROWS].astype(jnp.bfloat16)
+            lob[n, i : i + 1, :] = log[i * ROWS : (i + 1) * ROWS].T[0:1, :]
 
     lob[...] = jnp.zeros_like(lob)
+    sums_b[...] = jnp.ones_like(sums_b)
     for copy in loads:
         copy.wait()
     for copy in kvs:
         copy.wait_recv()
-    both(0, sa, ma, None, None, None)
+    both(0, sa, ma, None, None, None, None, None, None)
 
     last = 8 * units - 1
 
     def step(k, carry):
         n = 2 * k
-        before(n + 1)
-        both(n + 1, sb, mb, n, sa, ma)
+        before(k)
+        finish(jnp.maximum(n - 1, 0), low_b, sums_b, acc_b)
+        both(n + 1, sb, mb, n, sa, ma, low_a, sums_a, acc_a)
+        finish(n, low_a, sums_a, acc_a)
+        both(jnp.minimum(n + 2, last), sa, ma, n + 1, sb, mb, low_b, sums_b, acc_b)
+        after(n - 1)
         after(n)
-        before(jnp.minimum(n + 2, last + 1))
-        both(jnp.minimum(n + 2, last), sa, ma, n + 1, sb, mb)
-        after(n + 1)
         return carry
 
     lax.fori_loop(0, 4 * units, step, 0)
+    finish(last, low_b, sums_b, acc_b)
+    merge_send(5, units - 1, T3, (IN34, IN35), IN03, zp)
 
     for u in range(units):
         merge_send(6, u, T1, (IN16,), IN01, bwd)
@@ -470,6 +473,12 @@
             pltpu.VMEM((7 * units, 8, ROWS), f32),
             pltpu.VMEM((UROWS, keys), f32),
             pltpu.VMEM((UROWS, keys), f32),
+            pltpu.VMEM((UROWS, 128), f32),
+            pltpu.VMEM((UROWS, 128), f32),
+            pltpu.VMEM((UROWS, 128), f32),
+            pltpu.VMEM((UROWS, 128), f32),
+            pltpu.VMEM((UROWS, 128), f32),
+            pltpu.VMEM((UROWS, 128), f32),
             pltpu.VMEM((UROWS, 128), f32),
             pltpu.VMEM((UROWS, 128), f32),
             pltpu.SMEM((8, 4), jnp.int32),

time: 93.1 us -> 90.7 us (0.974)
  Pallas kernels: 88.6 us -> 85.9 us
    pallas_call x1, Pallas kernels: 88.6 us -> 85.9 us  [attend(): pl.pallas_call(functools.partial(attend_kernel, units), out_shape=jax.Sha...]
where the time goes in v3:
time: 90.7 us; the launch traced here: 88.9 us
  Pallas kernels  85.9 us (95%)
  local copies, waits for them, and re-layouts  3.01 us (3%)
    pallas_call x1, Pallas kernels, attend(): pl.pallas_call(functools.partial(attend_kernel, units), out_shape=jax.Sha...  85.9 us
    unnamed x2, local copies, waits for them, and re-layouts  3.01 us

profile of v3, /device:TPU:48, one launch (start us, length us, event | category | flops | bytes accessed | tf_op | source)
XLA Modules:
  0.0 88.9 jit_solution(11518669219657066818)
XLA Ops:
  0.0 1.3 %copy.10.lengths = s32[4,2]{1,0:T(4,128)} copy(s32[4,2]{0,1:T(2,128)} %param.14) | data formatting | bytes 64 | tf_op args[5]
  1.3 85.9 %attend.1 = bf16[2,128,512]{2,1,0:T(8,128)(2,1)} custom-call(s32[4,2]{1,0:T(4,128)} %copy.10.lengths, s32[4]{0:T(128)} %prompts.1, s32[16]{0:T(128)} %tiles.1, bf16[1,128,1024]{2,1,0:T(8,128)(2,1)} %q.1, bf16[1,128,128]{2,1,0:T(8,128)(2,1)} %ck.1, bf16[1,128,128]{2,1,0:T(8,128)(2,1)} %cv.1, bf16[2,1024,128]{2,1,0:T(8,128)(2,1)} %pk.1, ...), custom_call_target="tpu_custom_call" | custom-call | tf_op jit(solution)/shard_map/attend/pallas_call | solution.py:459
  87.2 1.7 %copy.12 = bf16[2,128,512]{2,1,0:T(8,128)(2,1)} copy(bf16[2,128,512]{2,1,0:T(8,128)(2,1)} %attend.1) | data formatting | bytes 524288

commit v4 on v3

--- a/solution.py
+++ b/solution.py
@@ -20,9 +20,19 @@
 UCOLS = HEADS_UNIT * WIDTH
 UROWS = HEADS_UNIT * ROWS
 CHUNK = 512
-
-PLACES = ((0, 0), (0, 1), (0, 3), (1, 1), (1, 2), (1, 3), (0, 2), (1, 0))
-T0, T2, T1, T5, T7, T4, T6, T3 = range(8)
+RELAYS1 = ((1, (0,)), (2, (1,)), (3, (2,)), (4, (3,)))
+RELAYS2 = ((5, (0, 1)), (6, (2,)), (7, (3,)))
+
+PLACES = ((0, 0), (0, 3), (1, 0), (1, 1), (1, 2), (1, 3), (0, 2), (0, 1))
+T0, T1, T3, T5, T7, T4, T6, T2 = range(8)
+
+
+def at(place, u, units):
+    if place in (T1, T3):
+        return units + 2 * u + place - T1
+    return place * units + u
+
+
 IN67, IN16, IN34, IN35, IN01, IN02, IN03 = range(7)
 
 
@@ -37,7 +47,7 @@
     kall, vall, ckb, cvb, qbuf, obuf, rbuf, lob, lrb, sa, sb, ma, mb, low_a, low_b, sums_a, sums_b, acc_a, acc_b, info,
     wbuf, abuf, pbuf, far_in, leaf_in, inter_in, zin, zout, fin, xout,
     load_sem, kv_send, kv_recv, q_send, q_recv, o_send, o_recv, l_send, l_recv,
-    a_send, a_recv, far_send, far_recv, leaf_send, leaf_recv, inter_send, inter_recv, z_send, z_recv, x_sem,
+    a_send, a_recv, far_recv, leaf_recv, inter_recv, z_recv, f_send, x_sem,
 ):
     me = lax.axis_index("seq")
     z, y, c = me // 8, (me // 2) % 4, me % 2
@@ -76,6 +86,8 @@
         pl.semaphore_signal(barrier, inc=1, device_id=peer, device_id_type=MESH)
     pl.semaphore_wait(barrier, 7)
 
+    last = 8 * units - 1
+
     def remote(src, dst, send, recv, to):
         return pltpu.make_async_remote_copy(
             src_ref=src, dst_ref=dst, send_sem=send, recv_sem=recv, device_id=to, device_id_type=MESH
@@ -83,8 +95,8 @@
 
     def kv_copies():
         return [
+            remote(pk, kall.at[:, pl.ds(kd, kd), :], kv_send.at[0], kv_recv.at[0], other),
             remote(ck.at[0], ckb.at[pl.ds(ROWS, ROWS), :], kv_send.at[2], kv_recv.at[2], other),
-            remote(pk, kall.at[:, pl.ds(kd, kd), :], kv_send.at[0], kv_recv.at[0], other),
             remote(pv, vall.at[:, pl.ds(kd, kd), :], kv_send.at[1], kv_recv.at[1], other),
             remote(cv.at[0], cvb.at[pl.ds(ROWS, ROWS), :], kv_send.at[3], kv_recv.at[3], other),
         ]
@@ -92,9 +104,9 @@
     wsend = remote(weight, wbuf.at[c], kv_send.at[4], kv_recv.at[4], other)
 
     def q_copy(number, u, place_from, place_to, to):
-        src = q.at[0, :, pl.ds(u * UCOLS, UCOLS)] if place_from is None else qbuf.at[place_from * units + u]
-        k = place_to * units + u
-        return remote(src, qbuf.at[k], q_send.at[number * units + u], q_recv.at[k], to)
+        src = q.at[0, :, pl.ds(u * UCOLS, UCOLS)] if place_from is None else qbuf.at[at(place_from, u, units)]
+        k = at(place_to, u, units)
+        return remote(src, qbuf.at[k], q_send.at[0], q_recv.at[k], to)
 
     sends0 = []
     for u in range(units):
@@ -110,8 +122,6 @@
         copy.start()
     for copy in sends0[3:]:
         copy.start()
-    wload.start()
-    wsend.start()
 
     mine, theirs = tiles[me], tiles[me + d]
     for place, (zf, steps) in enumerate(PLACES):
@@ -129,10 +139,10 @@
         pltpu.make_async_copy(buf.at[k], buf.at[k], sems.at[k]).wait()
 
     def o_copy(number, u, place, slot, to):
-        k, j = place * units + u, slot * units + u
+        k, j = at(place, u, units), slot * units + u
         return (
-            remote(obuf.at[k], rbuf.at[j], o_send.at[number * units + u], o_recv.at[j], to),
-            remote(lob.at[k], lrb.at[j], l_send.at[number * units + u], l_recv.at[j], to),
+            remote(obuf.at[k], rbuf.at[j], o_send.at[0], o_recv.at[j], to),
+            remote(lob.at[k], lrb.at[j], l_send.at[0], l_recv.at[j], to),
         )
 
     def send_out(number, u, place, slot, to):
@@ -140,7 +150,7 @@
             copy.start()
 
     def merged(u, place, slots):
-        k = place * units + u
+        k = at(place, u, units)
         js = [slot * units + u for slot in slots]
         for j in js:
             wait_in(rbuf, o_recv, j)
@@ -163,64 +173,50 @@
 
     def merge_send(number, u, place, slots, slot, to):
         o, log = merged(u, place, slots)
-        obuf[place * units + u] = o.astype(jnp.bfloat16)
-        lob[place * units + u] = log
+        obuf[at(place, u, units)] = o.astype(jnp.bfloat16)
+        lob[at(place, u, units)] = log
         send_out(number, u, place, slot, to)
 
     def relay1(u):
-        wait_in(qbuf, q_recv, T1 * units + u)
+        wait_in(qbuf, q_recv, at(T1, u, units))
         q_copy(3, u, T1, T6, fwd).start()
-        wait_in(qbuf, q_recv, T3 * units + u)
+        wait_in(qbuf, q_recv, at(T3, u, units))
         q_copy(4, u, T3, T4, fwd).start()
         q_copy(5, u, T3, T5, bwd).start()
 
     def relay2(u):
-        wait_in(qbuf, q_recv, T6 * units + u)
+        wait_in(qbuf, q_recv, at(T6, u, units))
         q_copy(6, u, T6, T7, zp).start()
 
     def before(k):
-        @pl.when(k < units)
-        def _():
-            relay1(k)
-
-        @pl.when((k >= units) & (k < 2 * units))
-        def _():
-            relay2(k - units)
+        for relays, relay in ((RELAYS1, relay1), (RELAYS2, relay2)):
+            for block, passed in relays:
+
+                @pl.when(k == block)
+                def _():
+                    for u in passed:
+                        relay(u)
 
         for ahead_by in (1, 2):
             n = 2 * k + ahead_by
-            place = n // units
-
-            @pl.when((place == T2) | (place == T5) | (place == T7) | (place == T4))
+
+            @pl.when(((n >= T5 * units) & (n < T6 * units)) | ((n >= T2 * units) & (n <= last)))
             def _():
                 wait_in(qbuf, q_recv, n)
 
     def after(n):
-        place, u = n // units, n % units
-
-        @pl.when(place == T2)
-        def _():
-            send_out(0, u, T2, IN02, fwd)
-
-        @pl.when(place == T5)
-        def _():
-            send_out(1, u, T5, IN35, fwd)
-
-        @pl.when(place == T7)
-        def _():
-            send_out(2, u, T7, IN67, zp)
-
-        @pl.when(place == T4)
-        def _():
-            send_out(3, u, T4, IN34, bwd)
-
-        @pl.when(place == T6)
-        def _():
-            merge_send(4, u, T6, (IN67,), IN16, bwd)
-
-        @pl.when(place == T3)
-        def _():
-            merge_send(5, u, T3, (IN34, IN35), IN03, zp)
+        def at_unit(first, action):
+            @pl.when((n >= first) & (n < first + units))
+            def _():
+                action(n - first)
+
+        at_unit(T5 * units, lambda u: send_out(1, u, T5, IN35, fwd))
+        at_unit(T7 * units, lambda u: send_out(2, u, T7, IN67, zp))
+        at_unit(T4 * units, lambda u: send_out(3, u, T4, IN34, bwd))
+        at_unit(T6 * units, lambda u: merge_send(4, u, T6, (IN67,), IN16, bwd))
+        at_unit(T6 * units + 2, lambda u: merge_send(5, u, T3, (IN34, IN35), IN03, zp))
+        at_unit(T2 * units, lambda u: send_out(0, u, T2, IN02, fwd))
+        at_unit(T2 * units + 1, lambda u: merge_send(6, u, T1, (IN16,), IN01, bwd))
 
     chunks = [(i * CHUNK, CHUNK) for i in range(2 * kd // CHUNK)]
     total_keys = 2 * kd
@@ -228,18 +224,22 @@
     def fold(op, x):
         parts = [x[:, i : i + 128] for i in range(0, x.shape[1], 128)]
         return functools.reduce(op, parts)
+
+    def place_of(n):
+        n = jnp.int32(n)
+        return jnp.where((n >= units) & (n < 3 * units), T1 + (n - units) % 2, n // units)
 
     def both(n1, s1, m1, n2, s2, m2, low2, sums2, acc2):
         first = n1 is not None
         second = n2 is not None
         if first:
-            place1 = n1 // units
+            place1 = place_of(n1)
             p1 = info[place1, 0]
             raw = qbuf[n1]
             query = jnp.concatenate([raw[:, i * WIDTH : (i + 1) * WIDTH] for i in range(HEADS_UNIT)], axis=0)
             peak = None
         if second:
-            p2 = info[n2 // units, 0]
+            p2 = info[place_of(n2), 0]
             low = jnp.broadcast_to(jnp.max(m2[...], axis=1, keepdims=True) * SCALE, (UROWS, 128))
             sums = jnp.zeros((UROWS, 128), jnp.float32)
             acc = jnp.zeros((UROWS, WIDTH), jnp.float32)
@@ -281,13 +281,17 @@
 
     lob[...] = jnp.zeros_like(lob)
     sums_b[...] = jnp.ones_like(sums_b)
-    for copy in loads:
-        copy.wait()
-    for copy in kvs:
-        copy.wait_recv()
+    for n in (0, 2, 4):
+        loads[n].wait()
+    kvs[0].wait_recv()
+    kvs[1].wait_recv()
     both(0, sa, ma, None, None, None, None, None, None)
-
-    last = 8 * units - 1
+    for n in (1, 3) + tuple(range(5, 4 + units)):
+        loads[n].wait()
+    kvs[2].wait_recv()
+    kvs[3].wait_recv()
+    wload.start()
+    wsend.start()
 
     def step(k, carry):
         n = 2 * k
@@ -302,15 +306,14 @@
 
     lax.fori_loop(0, 4 * units, step, 0)
     finish(last, low_b, sums_b, acc_b)
-    merge_send(5, units - 1, T3, (IN34, IN35), IN03, zp)
-
-    for u in range(units):
-        merge_send(6, u, T1, (IN16,), IN01, bwd)
+    send_out(0, units - 1, T2, IN02, fwd)
+    merge_send(6, units - 2, T1, (IN16,), IN01, bwd)
+    merge_send(6, units - 1, T1, (IN16,), IN01, bwd)
 
     def a_copy(number, u, place_from, place_to, to):
         k = place_to * units + u
         return remote(
-            abuf.at[place_from * units + u], abuf.at[k], a_send.at[number * units + u], a_recv.at[k], to
+            abuf.at[place_from * units + u], abuf.at[k], a_send.at[0], a_recv.at[k], to
         )
 
     def a_relay1(u):
@@ -325,7 +328,7 @@
         a_copy(6, u, T6, T7, zp).start()
 
     tile = tiles[me]
-    limit = lengths[tile // 4, tile // 2 % 2] - tile % 2 * ROWS
+    limit = lengths[tile // 2 % 2, tile // 4] - tile % 2 * ROWS
     live = lax.broadcasted_iota(jnp.int32, (ROWS, UCOLS), 0) < limit
     for u in range(units):
         o, _ = merged(u, T0, (IN02, IN03, IN01))
@@ -336,15 +339,15 @@
 
     def far_copy(zt, part, source):
         k = zt * 2 + part
-        return remote(pbuf.at[source * 2 + part], far_in.at[k], far_send.at[k], far_recv.at[k], xbwd)
+        return remote(pbuf.at[source * 2 + part], far_in.at[k], f_send.at[0], far_recv.at[k], xbwd)
 
     def leaf_copy(zt, part, source):
         k = zt * 2 + part
-        return remote(pbuf.at[source * 2 + part], leaf_in.at[k], leaf_send.at[k], leaf_recv.at[k], xfwd)
+        return remote(pbuf.at[source * 2 + part], leaf_in.at[k], f_send.at[0], leaf_recv.at[k], xfwd)
 
     def inter_copy(zt, part, source):
         k = zt * 2 + part
-        return remote(pbuf.at[source * 2 + part], inter_in.at[k], inter_send.at[k], inter_recv.at[k], xbwd)
+        return remote(pbuf.at[source * 2 + part], inter_in.at[k], f_send.at[0], inter_recv.at[k], xbwd)
 
     def project(place):
         zf, steps = PLACES[place]
@@ -370,6 +373,20 @@
         for u in range(units):
             wait_in(abuf, a_recv, place * units + u)
 
+    f32 = jnp.float32
+
+    def pass_on(place):
+        zf, steps = PLACES[place]
+        home = seq(zf, steps) // 2
+
+        @pl.when((home // 2 - x + d + 4) % 4 == 0)
+        def _():
+            for part in range(2):
+                k, m = home % 2 * 2 + part, home * 2 + part
+                wait_in(far_in, far_recv, k)
+                pbuf[m] = (pbuf[m].astype(f32) + far_in[k].astype(f32)).astype(jnp.bfloat16)
+                inter_copy(home % 2, part, home).start()
+
     wload.wait()
     wsend.wait_recv()
     project(T0)
@@ -379,24 +396,23 @@
     project(T3)
     settle(T2)
     project(T2)
+    pass_on(T0)
     for u in range(units):
         a_relay2(u)
     project(T6)
+    pass_on(T1)
+    pass_on(T3)
     settle(T5)
     project(T5)
+    pass_on(T2)
     settle(T4)
     project(T4)
+    pass_on(T6)
     settle(T7)
     project(T7)
-
-    f32 = jnp.float32
-    inter_home = (x - d + 4) % 4 * 2
-    for zt in (1 - zh, zh):
-        for part in range(2):
-            k, m = zt * 2 + part, (inter_home + zt) * 2 + part
-            wait_in(far_in, far_recv, k)
-            pbuf[m] = (pbuf[m].astype(f32) + far_in[k].astype(f32)).astype(jnp.bfloat16)
-            inter_copy(zt, part, inter_home + zt).start()
+    pass_on(T5)
+    pass_on(T4)
+    pass_on(T7)
 
     def column_sum(zt, part):
         k = zt * 2 + part
@@ -406,7 +422,7 @@
         return here + leaf_in[k].astype(f32) + inter_in[k].astype(f32)
 
     def z_copy(part):
-        return remote(zout.at[part], zin.at[part], z_send.at[part], z_recv.at[part], zhp)
+        return remote(zout.at[part], zin.at[part], f_send.at[0], z_recv.at[part], zhp)
 
     for part in range(2):
         zout[part] = column_sum(1 - zh, part).astype(jnp.bfloat16)
@@ -421,30 +437,13 @@
     out[c] = (fin[c] + zin[c].astype(f32)).astype(jnp.bfloat16)
     last_copy.wait()
 
-    for copy in sends0 + kvs + [wsend]:
+    for copy in kvs + [wsend]:
         copy.wait_send()
-    for part in range(2):
-        z_copy(part).wait_send()
-        for zt in range(2):
-            far_copy(zt, part, 0).wait_send()
-            leaf_copy(zt, part, 0).wait_send()
-            inter_copy(zt, part, 0).wait_send()
-
-    def drain(u, carry):
-        for make in (q_copy, a_copy):
-            for number, src, dst, to in ((3, T1, T6, fwd), (4, T3, T4, fwd), (5, T3, T5, bwd), (6, T6, T7, zp)):
-                make(number, u, src, dst, to).wait_send()
-        for number, dst, to in ((0, T1, fwd), (1, T2, bwd), (2, T3, zp)):
-            a_copy(number, u, T0, dst, to).wait_send()
-        for number, place, slot, to in (
-            (0, T2, IN02, fwd), (1, T5, IN35, fwd), (2, T7, IN67, zp), (3, T4, IN34, bwd),
-            (4, T6, IN16, bwd), (5, T3, IN03, zp), (6, T1, IN01, bwd),
-        ):
-            for copy in o_copy(number, u, place, slot, to):
-                copy.wait_send()
-        return carry
-
-    lax.fori_loop(0, units, drain, 0)
+    for buf, sem in ((qbuf, q_send), (obuf, o_send), (lob, l_send), (abuf, a_send)):
+        whole = buf.at[pl.ds(0, 7 * units)]
+        pltpu.make_async_copy(whole, whole, sem.at[0]).wait()
+    whole = pbuf.at[pl.ds(0, 14)]
+    pltpu.make_async_copy(whole, whole, f_send.at[0]).wait()
 
 
 def attend(lengths, prompts, tiles, q, ck, cv, pk, pv, weight):
@@ -495,22 +494,19 @@
             dma((5 + units,)),
             dma((5,)),
             dma((5,)),
+            dma((1,)),
+            dma((8 * units,)),
+            dma((1,)),
             dma((7 * units,)),
-            dma((8 * units,)),
+            dma((1,)),
             dma((7 * units,)),
-            dma((7 * units,)),
-            dma((7 * units,)),
-            dma((7 * units,)),
-            dma((7 * units,)),
+            dma((1,)),
             dma((8 * units,)),
             dma((4,)),
             dma((4,)),
             dma((4,)),
-            dma((4,)),
-            dma((4,)),
-            dma((4,)),
             dma((2,)),
-            dma((2,)),
+            dma((1,)),
             dma((2,)),
         ],
         compiler_params=pltpu.CompilerParams(
@@ -521,7 +517,7 @@
 
 
 def local(q, ck, cv, pk, pv, lengths, prompts, tiles, weight):
-    return attend(lengths, prompts, tiles, q, ck, cv, pk, pv, weight)
+    return attend(lengths.T, prompts, tiles, q, ck, cv, pk, pv, weight)
 
 
 def solution(mesh):

time: 90.7 us -> 92.9 us (1.024)
  Pallas kernels: 85.9 us -> 89.5 us
  local copies, waits for them, and re-layouts: 3.01 us -> 1.67 us
    pallas_call x1, Pallas kernels: 85.9 us -> 89.5 us  [attend(): pl.pallas_call(functools.partial(attend_kernel, units), out_shape=jax.Sha...]
    unnamed x2 -> x1, local copies, waits for them, and re-layouts: 3.01 us -> 1.67 us
where the time goes in v4:
time: 92.9 us; the launch traced here: 91.2 us
  Pallas kernels  89.5 us (96%)
  local copies, waits for them, and re-layouts  1.67 us (2%)
    pallas_call x1, Pallas kernels, attend(): pl.pallas_call(functools.partial(attend_kernel, units), out_shape=jax.Sha...  89.5 us

profile of v4, /device:TPU:48, one launch (start us, length us, event | category | flops | bytes accessed | tf_op | source)
XLA Modules:
  0.0 91.2 jit_solution(3700874748009382525)
XLA Ops:
  0.0 89.5 %attend.1 = bf16[2,128,512]{2,1,0:T(8,128)(2,1)} custom-call(s32[2,4]{1,0:T(2,128)} %bitcast.1, s32[4]{0:T(128)} %prompts.1, s32[16]{0:T(128)} %tiles.1, bf16[1,128,1024]{2,1,0:T(8,128)(2,1)} %q.1, bf16[1,128,128]{2,1,0:T(8,128)(2,1)} %ck.1, bf16[1,128,128]{2,1,0:T(8,128)(2,1)} %cv.1, bf16[2,1024,128]{2,1,0:T(8,128)(2,1)} %pk.1, bf16[2,1024,128]{2,1,0:T(8,128)(2,1)} %pv.1, ...), custom_call_target="tpu_custom_call" | custom-call | tf_op jit(solution)/shard_map/attend/pallas_call | solution.py:458
  89.5 1.7 %copy.11 = bf16[2,128,512]{2,1,0:T(8,128)(2,1)} copy(bf16[2,128,512]{2,1,0:T(8,128)(2,1)} %attend.1) | data formatting | bytes 524288

commit v5 on v4

--- a/solution.py
+++ b/solution.py
@@ -20,17 +20,24 @@
 UCOLS = HEADS_UNIT * WIDTH
 UROWS = HEADS_UNIT * ROWS
 CHUNK = 512
+PIECES = 4
+PIECES = 4
 RELAYS1 = ((1, (0,)), (2, (1,)), (3, (2,)), (4, (3,)))
-RELAYS2 = ((5, (0, 1)), (6, (2,)), (7, (3,)))
-
-PLACES = ((0, 0), (0, 3), (1, 0), (1, 1), (1, 2), (1, 3), (0, 2), (0, 1))
-T0, T1, T3, T5, T7, T4, T6, T2 = range(8)
+RELAYS2 = ((4, (0,)), (5, (1,)), (6, (2,)), (7, (3,)))
+
+PLACES = ((0, 0), (0, 1), (1, 0), (1, 1), (1, 3), (1, 2), (0, 2), (0, 3))
+T0, T2, T3, T5, T4, T7, T6, T1 = range(8)
+UNITS = 4
+ORDER = (
+    (T0, 0), (T0, 1), (T0, 2), (T2, 0), (T3, 0), (T2, 1), (T3, 1), (T1, 0),
+    (T1, 1), (T5, 0), (T5, 1), (T4, 0), (T4, 1), (T7, 0), (T6, 0), (T7, 1),
+    (T6, 1), (T7, 2), (T7, 3), (T4, 2), (T4, 3), (T6, 2), (T6, 3), (T5, 2),
+    (T5, 3), (T1, 2), (T1, 3), (T3, 2), (T3, 3), (T2, 2), (T2, 3), (T0, 3),
+)
 
 
 def at(place, u, units):
-    if place in (T1, T3):
-        return units + 2 * u + place - T1
-    return place * units + u
+    return ORDER.index((place, u))
 
 
 IN67, IN16, IN34, IN35, IN01, IN02, IN03 = range(7)
@@ -47,7 +54,7 @@
     kall, vall, ckb, cvb, qbuf, obuf, rbuf, lob, lrb, sa, sb, ma, mb, low_a, low_b, sums_a, sums_b, acc_a, acc_b, info,
     wbuf, abuf, pbuf, far_in, leaf_in, inter_in, zin, zout, fin, xout,
     load_sem, kv_send, kv_recv, q_send, q_recv, o_send, o_recv, l_send, l_recv,
-    a_send, a_recv, far_recv, leaf_recv, inter_recv, z_recv, f_send, x_sem,
+    a_send, a_recv, far_recv, leaf_recv, inter_recv, z_recv, f_send, x_send, x_recv,
 ):
     me = lax.axis_index("seq")
     z, y, c = me // 8, (me // 2) % 4, me % 2
@@ -74,7 +81,7 @@
         pltpu.make_async_copy(ck.at[0], ckb.at[pl.ds(0, ROWS), :], load_sem.at[2]),
         pltpu.make_async_copy(cv.at[0], cvb.at[pl.ds(0, ROWS), :], load_sem.at[3]),
     ] + [
-        pltpu.make_async_copy(q.at[0, :, pl.ds(u * UCOLS, UCOLS)], qbuf.at[u], load_sem.at[4 + u])
+        pltpu.make_async_copy(q.at[0, :, pl.ds(u * UCOLS, UCOLS)], qbuf.at[at(T0, u, units)], load_sem.at[4 + u])
         for u in range(units)
     ]
     wload = pltpu.make_async_copy(weight, wbuf.at[c], load_sem.at[4 + units])
@@ -126,10 +133,15 @@
     mine, theirs = tiles[me], tiles[me + d]
     for place, (zf, steps) in enumerate(PLACES):
         tile = tiles[seq(zf, steps)]
-        info[place, 0] = prompts[tile // 4]
-        for k, held in enumerate((mine, theirs)):
-            gap = (tile % 2 - held % 2) * ROWS
-            info[place, 1 + k] = jnp.where(tile // 2 == held // 2, gap, -4 * ROWS)
+        prompt = prompts[tile // 4]
+        reach = [
+            jnp.where(tile // 2 == held // 2, (tile % 2 - held % 2) * ROWS, -4 * ROWS) for held in (mine, theirs)
+        ]
+        for u in range(units):
+            n = at(place, u, units)
+            info[n, 0] = prompt
+            info[n, 1] = reach[0]
+            info[n, 2] = reach[1]
 
     ahead = lax.broadcasted_iota(jnp.int32, (UROWS, ROWS), 1) - (
         lax.broadcasted_iota(jnp.int32, (UROWS, ROWS), 0) % ROWS
@@ -188,35 +200,94 @@
         wait_in(qbuf, q_recv, at(T6, u, units))
         q_copy(6, u, T6, T7, zp).start()
 
-    def before(k):
-        for relays, relay in ((RELAYS1, relay1), (RELAYS2, relay2)):
-            for block, passed in relays:
-
-                @pl.when(k == block)
+    def run_at(k, table):
+        def choose(blocks):
+            if len(blocks) == 1:
+
+                @pl.when(k == blocks[0])
                 def _():
-                    for u in passed:
-                        relay(u)
-
-        for ahead_by in (1, 2):
-            n = 2 * k + ahead_by
-
-            @pl.when(((n >= T5 * units) & (n < T6 * units)) | ((n >= T2 * units) & (n <= last)))
-            def _():
-                wait_in(qbuf, q_recv, n)
-
-    def after(n):
-        def at_unit(first, action):
-            @pl.when((n >= first) & (n < first + units))
-            def _():
-                action(n - first)
-
-        at_unit(T5 * units, lambda u: send_out(1, u, T5, IN35, fwd))
-        at_unit(T7 * units, lambda u: send_out(2, u, T7, IN67, zp))
-        at_unit(T4 * units, lambda u: send_out(3, u, T4, IN34, bwd))
-        at_unit(T6 * units, lambda u: merge_send(4, u, T6, (IN67,), IN16, bwd))
-        at_unit(T6 * units + 2, lambda u: merge_send(5, u, T3, (IN34, IN35), IN03, zp))
-        at_unit(T2 * units, lambda u: send_out(0, u, T2, IN02, fwd))
-        at_unit(T2 * units + 1, lambda u: merge_send(6, u, T1, (IN16,), IN01, bwd))
+                    for action in table[blocks[0]]:
+                        action()
+
+            else:
+                middle = len(blocks) // 2
+                lax.cond(
+                    k < blocks[middle], lambda: choose(blocks[:middle]), lambda: choose(blocks[middle:])
+                )
+
+        choose(sorted(table))
+
+    ahead_of = {}
+    for block, u in ((1, 0), (2, 1), (3, 2), (4, 3)):
+        ahead_of.setdefault(block, []).append(functools.partial(relay1, u))
+    for block, u in ((4, 0), (5, 1), (6, 2), (7, 3)):
+        ahead_of.setdefault(block, []).append(functools.partial(relay2, u))
+    for n, (place, u) in enumerate(ORDER):
+        if place in (T2, T5, T4, T7):
+            ahead_of.setdefault((n - 1) // 2, []).append(functools.partial(wait_in, qbuf, q_recv, n))
+
+    def leaf_out(place, u):
+        number, slot, to = {T2: (0, IN02, fwd), T5: (1, IN35, fwd), T7: (2, IN67, zp), T4: (3, IN34, bwd)}[place]
+        send_out(number, u, place, slot, to)
+
+    def merge_out(place, u):
+        number, slots, slot, to = {
+            T6: (4, (IN67,), IN16, bwd),
+            T3: (5, (IN34, IN35), IN03, zp),
+            T1: (6, (IN16,), IN01, bwd),
+        }[place]
+        merge_send(number, u, place, slots, slot, to)
+
+    def a_copy(number, u, place_from, place_to, to):
+        k = place_to * units + u
+        return remote(
+            abuf.at[place_from * units + u], abuf.at[k], a_send.at[0], a_recv.at[k], to
+        )
+
+    def a_relay1(u):
+        wait_in(abuf, a_recv, T3 * units + u)
+        a_copy(5, u, T3, T5, bwd).start()
+        if u >= units // 2:
+            a_copy(1, u, T0, T2, bwd).start()
+        a_copy(4, u, T3, T4, fwd).start()
+        wait_in(abuf, a_recv, T1 * units + u)
+        a_copy(3, u, T1, T6, fwd).start()
+
+    def a_relay2(u):
+        wait_in(abuf, a_recv, T6 * units + u)
+        a_copy(6, u, T6, T7, zp).start()
+
+    tile = tiles[me]
+    limit = lengths[tile // 2 % 2, tile // 4] - tile % 2 * ROWS
+    live = lax.broadcasted_iota(jnp.int32, (ROWS, UCOLS), 0) < limit
+    def own_attention(u):
+        o, _ = merged(u, T0, (IN02, IN03, IN01))
+        abuf[T0 * units + u] = jnp.where(live, o, 0.0).astype(jnp.bfloat16)
+        a_copy(0, u, T0, T1, fwd).start()
+        if u < units // 2:
+            a_copy(1, u, T0, T2, bwd).start()
+        a_copy(2, u, T0, T3, zp).start()
+
+    done_after = {
+        block: [functools.partial(action, *args) for action, *args in actions]
+        for block, actions in {
+            2: [(leaf_out, T2, 0)],
+            3: [(leaf_out, T2, 1)],
+            5: [(leaf_out, T5, 0), (leaf_out, T5, 1)],
+            6: [(leaf_out, T4, 0), (leaf_out, T4, 1)],
+            7: [(leaf_out, T7, 0)],
+            8: [(leaf_out, T7, 1)],
+            9: [(leaf_out, T7, 2), (leaf_out, T7, 3), (merge_out, T6, 0)],
+            10: [(merge_out, T6, 1), (merge_out, T3, 0), (leaf_out, T4, 2), (leaf_out, T4, 3)],
+            11: [(merge_out, T1, 0), (merge_out, T3, 1)],
+            12: [(merge_out, T1, 1), (merge_out, T6, 2), (merge_out, T6, 3), (leaf_out, T5, 2), (leaf_out, T5, 3)],
+            13: [(own_attention, 0)],
+            14: [(own_attention, 1), (merge_out, T1, 2), (merge_out, T1, 3), (merge_out, T3, 2)],
+            15: [(leaf_out, T2, 2), (leaf_out, T2, 3), (merge_out, T3, 3)],
+        }.items()
+    }
+    for block, actions in ahead_of.items():
+        done_after.setdefault(block - 1, []).extend(actions)
 
     chunks = [(i * CHUNK, CHUNK) for i in range(2 * kd // CHUNK)]
     total_keys = 2 * kd
@@ -224,22 +295,17 @@
     def fold(op, x):
         parts = [x[:, i : i + 128] for i in range(0, x.shape[1], 128)]
         return functools.reduce(op, parts)
-
-    def place_of(n):
-        n = jnp.int32(n)
-        return jnp.where((n >= units) & (n < 3 * units), T1 + (n - units) % 2, n // units)
 
     def both(n1, s1, m1, n2, s2, m2, low2, sums2, acc2):
         first = n1 is not None
         second = n2 is not None
         if first:
-            place1 = place_of(n1)
-            p1 = info[place1, 0]
+            p1 = info[n1, 0]
             raw = qbuf[n1]
             query = jnp.concatenate([raw[:, i * WIDTH : (i + 1) * WIDTH] for i in range(HEADS_UNIT)], axis=0)
             peak = None
         if second:
-            p2 = info[place_of(n2), 0]
+            p2 = info[n2, 0]
             low = jnp.broadcast_to(jnp.max(m2[...], axis=1, keepdims=True) * SCALE, (UROWS, 128))
             sums = jnp.zeros((UROWS, 128), jnp.float32)
             acc = jnp.zeros((UROWS, WIDTH), jnp.float32)
@@ -251,7 +317,7 @@
                 if own:
                     s = jnp.concatenate(
                         [
-                            jnp.where(ahead <= info[place1, 1 + k], s[:, k * ROWS : (k + 1) * ROWS], VERY_LOW)
+                            jnp.where(ahead <= info[n1, 1 + k], s[:, k * ROWS : (k + 1) * ROWS], VERY_LOW)
                             for k in range(2)
                         ],
                         axis=1,
@@ -295,159 +361,141 @@
 
     def step(k, carry):
         n = 2 * k
-        before(k)
         finish(jnp.maximum(n - 1, 0), low_b, sums_b, acc_b)
         both(n + 1, sb, mb, n, sa, ma, low_a, sums_a, acc_a)
         finish(n, low_a, sums_a, acc_a)
         both(jnp.minimum(n + 2, last), sa, ma, n + 1, sb, mb, low_b, sums_b, acc_b)
-        after(n - 1)
-        after(n)
+        run_at(k, done_after)
         return carry
 
     lax.fori_loop(0, 4 * units, step, 0)
     finish(last, low_b, sums_b, acc_b)
-    send_out(0, units - 1, T2, IN02, fwd)
-    merge_send(6, units - 2, T1, (IN16,), IN01, bwd)
-    merge_send(6, units - 1, T1, (IN16,), IN01, bwd)
-
-    def a_copy(number, u, place_from, place_to, to):
-        k = place_to * units + u
-        return remote(
-            abuf.at[place_from * units + u], abuf.at[k], a_send.at[0], a_recv.at[k], to
-        )
-
-    def a_relay1(u):
-        wait_in(abuf, a_recv, T1 * units + u)
-        a_copy(3, u, T1, T6, fwd).start()
-        wait_in(abuf, a_recv, T3 * units + u)
-        a_copy(4, u, T3, T4, fwd).start()
-        a_copy(5, u, T3, T5, bwd).start()
-
-    def a_relay2(u):
-        wait_in(abuf, a_recv, T6 * units + u)
-        a_copy(6, u, T6, T7, zp).start()
-
-    tile = tiles[me]
-    limit = lengths[tile // 2 % 2, tile // 4] - tile % 2 * ROWS
-    live = lax.broadcasted_iota(jnp.int32, (ROWS, UCOLS), 0) < limit
-    for u in range(units):
-        o, _ = merged(u, T0, (IN02, IN03, IN01))
-        abuf[T0 * units + u] = jnp.where(live, o, 0.0).astype(jnp.bfloat16)
-        a_copy(0, u, T0, T1, fwd).start()
-        a_copy(1, u, T0, T2, bwd).start()
-        a_copy(2, u, T0, T3, zp).start()
-
-    def far_copy(zt, part, source):
-        k = zt * 2 + part
-        return remote(pbuf.at[source * 2 + part], far_in.at[k], f_send.at[0], far_recv.at[k], xbwd)
-
-    def leaf_copy(zt, part, source):
-        k = zt * 2 + part
-        return remote(pbuf.at[source * 2 + part], leaf_in.at[k], f_send.at[0], leaf_recv.at[k], xfwd)
-
-    def inter_copy(zt, part, source):
-        k = zt * 2 + part
-        return remote(pbuf.at[source * 2 + part], inter_in.at[k], f_send.at[0], inter_recv.at[k], xbwd)
+
+    a_relay1(0)
+    a_relay1(1)
+    own_attention(2)
+    own_attention(3)
+
+    f32 = jnp.float32
+    half = ROWS // 2
+
+    def piece_of(i):
+        return (i + 2 * (1 - c)) % PIECES
+
+    def x_copy(buf, sems, zt, piece, source, to):
+        k = zt * PIECES + piece
+        return remote(pbuf.at[source * PIECES + piece], buf.at[k], f_send.at[0], sems.at[k], to)
 
     def project(place):
         zf, steps = PLACES[place]
         home = seq(zf, steps) // 2
         rows = jnp.concatenate([abuf[place * units + u] for u in range(units)], axis=1)
+        gap = (home // 2 - x + 4) % 4
         for part in range(2):
-            pbuf[home * 2 + part] = jnp.dot(rows, wbuf[part], preferred_element_type=jnp.float32).astype(
-                jnp.bfloat16
-            )
-        gap = (home // 2 - x + 4) % 4
-
-        @pl.when(gap == 2)
-        def _():
-            for part in range(2):
-                far_copy(home % 2, part, home).start()
-
-        @pl.when(gap == (d + 4) % 4)
-        def _():
-            for part in range(2):
-                leaf_copy(home % 2, part, home).start()
+            r = jnp.dot(rows, wbuf[part], preferred_element_type=f32).astype(jnp.bfloat16)
+            for i in range(2):
+                pbuf[home * PIECES + part * 2 + i] = r[i * half : (i + 1) * half]
+        for i in range(PIECES):
+            piece = piece_of(i)
+
+            @pl.when(gap == 2)
+            def _():
+                x_copy(far_in, far_recv, home % 2, piece, home, xbwd).start()
+
+            @pl.when(gap == (d + 4) % 4)
+            def _():
+                x_copy(leaf_in, leaf_recv, home % 2, piece, home, xfwd).start()
 
     def settle(place):
         for u in range(units):
             wait_in(abuf, a_recv, place * units + u)
 
-    f32 = jnp.float32
-
     def pass_on(place):
         zf, steps = PLACES[place]
         home = seq(zf, steps) // 2
 
         @pl.when((home // 2 - x + d + 4) % 4 == 0)
         def _():
-            for part in range(2):
-                k, m = home % 2 * 2 + part, home * 2 + part
+            for i in range(PIECES):
+                piece = piece_of(i)
+                k, m = home % 2 * PIECES + piece, home * PIECES + piece
                 wait_in(far_in, far_recv, k)
                 pbuf[m] = (pbuf[m].astype(f32) + far_in[k].astype(f32)).astype(jnp.bfloat16)
-                inter_copy(home % 2, part, home).start()
+                x_copy(inter_in, inter_recv, home % 2, piece, home, xbwd).start()
 
     wload.wait()
     wsend.wait_recv()
     project(T0)
-    for u in range(units):
-        a_relay1(u)
+    a_relay2(0)
+    a_relay2(1)
+    a_relay1(2)
+    a_relay1(3)
+    project(T3)
     project(T1)
-    project(T3)
+    pass_on(T0)
+    settle(T5)
+    project(T5)
     settle(T2)
     project(T2)
-    pass_on(T0)
-    for u in range(units):
-        a_relay2(u)
-    project(T6)
-    pass_on(T1)
-    pass_on(T3)
-    settle(T5)
-    project(T5)
-    pass_on(T2)
+    a_relay2(2)
+    a_relay2(3)
     settle(T4)
     project(T4)
-    pass_on(T6)
+    project(T6)
+    pass_on(T3)
+    pass_on(T1)
     settle(T7)
     project(T7)
     pass_on(T5)
+    pass_on(T2)
     pass_on(T4)
+    pass_on(T6)
     pass_on(T7)
 
-    def column_sum(zt, part):
-        k = zt * 2 + part
+    def column_sum(zt, piece):
+        k = zt * PIECES + piece
         wait_in(leaf_in, leaf_recv, k)
         wait_in(inter_in, inter_recv, k)
-        here = pbuf[(x * 2 + zt) * 2 + part].astype(f32)
+        here = pbuf[(x * 2 + zt) * PIECES + piece].astype(f32)
         return here + leaf_in[k].astype(f32) + inter_in[k].astype(f32)
 
-    def z_copy(part):
-        return remote(zout.at[part], zin.at[part], f_send.at[0], z_recv.at[part], zhp)
-
-    for part in range(2):
-        zout[part] = column_sum(1 - zh, part).astype(jnp.bfloat16)
-        z_copy(part).start()
-    for part in range(2):
-        fin[part] = column_sum(zh, part)
-    for part in range(2):
-        wait_in(zin, z_recv, part)
-    xout[...] = (fin[1 - c] + zin[1 - c].astype(f32)).astype(jnp.bfloat16)
-    last_copy = remote(xout, out.at[c], x_sem.at[0], x_sem.at[1], other)
-    last_copy.start()
-    out[c] = (fin[c] + zin[c].astype(f32)).astype(jnp.bfloat16)
-    last_copy.wait()
+    def z_copy(piece):
+        return remote(zout.at[piece], zin.at[piece], f_send.at[0], z_recv.at[piece], zhp)
+
+    for i in range(PIECES):
+        piece = piece_of(i)
+        zout[piece] = column_sum(1 - zh, piece).astype(jnp.bfloat16)
+        z_copy(piece).start()
+    for i in range(PIECES):
+        piece = piece_of(i)
+        fin[piece] = column_sum(zh, piece)
+    last_copies = []
+    for i in range(2):
+        piece = (1 - c) * 2 + i
+        wait_in(zin, z_recv, piece)
+        xout[i] = (fin[piece] + zin[piece].astype(f32)).astype(jnp.bfloat16)
+        rows = pl.ds(i * half, half)
+        last_copies.append(remote(xout.at[i], out.at[c, rows], x_send.at[i], x_recv.at[i], other))
+        last_copies[-1].start()
+    for i in range(2):
+        piece = c * 2 + i
+        wait_in(zin, z_recv, piece)
+        out[c, i * half : (i + 1) * half] = (fin[piece] + zin[piece].astype(f32)).astype(jnp.bfloat16)
+    for copy in last_copies:
+        copy.wait()
 
     for copy in kvs + [wsend]:
         copy.wait_send()
     for buf, sem in ((qbuf, q_send), (obuf, o_send), (lob, l_send), (abuf, a_send)):
         whole = buf.at[pl.ds(0, 7 * units)]
         pltpu.make_async_copy(whole, whole, sem.at[0]).wait()
-    whole = pbuf.at[pl.ds(0, 14)]
+    whole = pbuf.at[pl.ds(0, 7 * PIECES)]
     pltpu.make_async_copy(whole, whole, f_send.at[0]).wait()
 
 
 def attend(lengths, prompts, tiles, q, ck, cv, pk, pv, weight):
     units = q.shape[2] // UCOLS
+    assert units == UNITS
     kd = pk.shape[1]
     cols = weight.shape[1]
     keys = 2 * kd + 2 * ROWS
@@ -480,17 +528,17 @@
             pltpu.VMEM((UROWS, 128), f32),
             pltpu.VMEM((UROWS, 128), f32),
             pltpu.VMEM((UROWS, 128), f32),
-            pltpu.SMEM((8, 4), jnp.int32),
+            pltpu.SMEM((8 * units, 4), jnp.int32),
             pltpu.VMEM((2,) + weight.shape, bf),
             pltpu.VMEM((8 * units, ROWS, UCOLS), bf),
-            pltpu.VMEM((16, ROWS, cols), bf),
-            pltpu.VMEM((4, ROWS, cols), bf),
-            pltpu.VMEM((4, ROWS, cols), bf),
-            pltpu.VMEM((4, ROWS, cols), bf),
-            pltpu.VMEM((2, ROWS, cols), bf),
-            pltpu.VMEM((2, ROWS, cols), bf),
-            pltpu.VMEM((2, ROWS, cols), f32),
-            pltpu.VMEM((ROWS, cols), bf),
+            pltpu.VMEM((8 * PIECES, ROWS // 2, cols), bf),
+            pltpu.VMEM((2 * PIECES, ROWS // 2, cols), bf),
+            pltpu.VMEM((2 * PIECES, ROWS // 2, cols), bf),
+            pltpu.VMEM((2 * PIECES, ROWS // 2, cols), bf),
+            pltpu.VMEM((PIECES, ROWS // 2, cols), bf),
+            pltpu.VMEM((PIECES, ROWS // 2, cols), bf),
+            pltpu.VMEM((PIECES, ROWS // 2, cols), f32),
+            pltpu.VMEM((2, ROWS // 2, cols), bf),
             dma((5 + units,)),
             dma((5,)),
             dma((5,)),
@@ -502,11 +550,12 @@
             dma((7 * units,)),
             dma((1,)),
             dma((8 * units,)),
-            dma((4,)),
-            dma((4,)),
-            dma((4,)),
+            dma((2 * PIECES,)),
+            dma((2 * PIECES,)),
+            dma((2 * PIECES,)),
+            dma((PIECES,)),
+            dma((1,)),
             dma((2,)),
-            dma((1,)),
             dma((2,)),
         ],
         compiler_params=pltpu.CompilerParams(

time: 92.9 us -> 86.3 us (0.929)
  Pallas kernels: 89.5 us -> 83 us
    pallas_call x1, Pallas kernels: 89.5 us -> 83 us  [attend(): pl.pallas_call(functools.partial(attend_kernel, units), out_shape=jax.Sha...]
where the time goes in v5:
time: 86.3 us; the launch traced here: 84.7 us
  Pallas kernels  83 us (96%)
  local copies, waits for them, and re-layouts  1.67 us (2%)
    pallas_call x1, Pallas kernels, attend(): pl.pallas_call(functools.partial(attend_kernel, units), out_shape=jax.Sha...  83 us

profile of v5, /device:TPU:48, one launch (start us, length us, event | category | flops | bytes accessed | tf_op | source)
XLA Modules:
  0.0 84.7 jit_solution(2953722576921266174)
XLA Ops:
  0.0 83.0 %attend.1 = bf16[2,128,512]{2,1,0:T(8,128)(2,1)} custom-call(s32[2,4]{1,0:T(2,128)} %bitcast.1, s32[4]{0:T(128)} %prompts.1, s32[16]{0:T(128)} %tiles.1, bf16[1,128,1024]{2,1,0:T(8,128)(2,1)} %q.1, bf16[1,128,128]{2,1,0:T(8,128)(2,1)} %ck.1, bf16[1,128,128]{2,1,0:T(8,128)(2,1)} %cv.1, bf16[2,1024,128]{2,1,0:T(8,128)(2,1)} %pk.1, bf16[2,1024,128]{2,1,0:T(8,128)(2,1)} %pv.1, ...), custom_call_target="tpu_custom_call" | custom-call | tf_op jit(solution)/shard_map/attend/pallas_call | solution.py:506
  83.0 1.7 %copy.11 = bf16[2,128,512]{2,1,0:T(8,128)(2,1)} copy(bf16[2,128,512]{2,1,0:T(8,128)(2,1)} %attend.1) | data formatting | bytes 524288

commit v6 on v5

--- a/solution.py
+++ b/solution.py
@@ -19,7 +19,7 @@
 HEADS_UNIT = 2
 UCOLS = HEADS_UNIT * WIDTH
 UROWS = HEADS_UNIT * ROWS
-CHUNK = 512
+CHUNK = 256
 PIECES = 4
 PIECES = 4
 RELAYS1 = ((1, (0,)), (2, (1,)), (3, (2,)), (4, (3,)))
@@ -31,7 +31,7 @@
 ORDER = (
     (T0, 0), (T0, 1), (T0, 2), (T2, 0), (T3, 0), (T2, 1), (T3, 1), (T1, 0),
     (T1, 1), (T5, 0), (T5, 1), (T4, 0), (T4, 1), (T7, 0), (T6, 0), (T7, 1),
-    (T6, 1), (T7, 2), (T7, 3), (T4, 2), (T4, 3), (T6, 2), (T6, 3), (T5, 2),
+    (T6, 1), (T4, 2), (T4, 3), (T7, 2), (T7, 3), (T6, 2), (T6, 3), (T5, 2),
     (T5, 3), (T1, 2), (T1, 3), (T3, 2), (T3, 3), (T2, 2), (T2, 3), (T0, 3),
 )
 
@@ -277,13 +277,13 @@
             6: [(leaf_out, T4, 0), (leaf_out, T4, 1)],
             7: [(leaf_out, T7, 0)],
             8: [(leaf_out, T7, 1)],
-            9: [(leaf_out, T7, 2), (leaf_out, T7, 3), (merge_out, T6, 0)],
-            10: [(merge_out, T6, 1), (merge_out, T3, 0), (leaf_out, T4, 2), (leaf_out, T4, 3)],
+            9: [(leaf_out, T4, 2), (leaf_out, T4, 3), (merge_out, T6, 0)],
+            10: [(leaf_out, T7, 2), (leaf_out, T7, 3), (merge_out, T6, 1), (merge_out, T3, 0)],
             11: [(merge_out, T1, 0), (merge_out, T3, 1)],
-            12: [(merge_out, T1, 1), (merge_out, T6, 2), (merge_out, T6, 3), (leaf_out, T5, 2), (leaf_out, T5, 3)],
+            12: [(merge_out, T1, 1), (leaf_out, T5, 2), (leaf_out, T5, 3), (merge_out, T6, 2), (merge_out, T6, 3)],
             13: [(own_attention, 0)],
-            14: [(own_attention, 1), (merge_out, T1, 2), (merge_out, T1, 3), (merge_out, T3, 2)],
-            15: [(leaf_out, T2, 2), (leaf_out, T2, 3), (merge_out, T3, 3)],
+            14: [(merge_out, T3, 2), (own_attention, 1)],
+            15: [(leaf_out, T2, 2), (leaf_out, T2, 3), (merge_out, T3, 3), (merge_out, T1, 2), (merge_out, T1, 3)],
         }.items()
     }
     for block, actions in ahead_of.items():

time: 86.3 us -> 85.1 us (0.986); the launches traced: 84.7 us -> 84.7 us
  no operation moved by 1% of the time
where the time goes in v6:
time: 85.1 us; the launch traced here: 84.7 us
  Pallas kernels  83 us (98%)
  local copies, waits for them, and re-layouts  1.67 us (2%)
    pallas_call x1, Pallas kernels, attend(): pl.pallas_call(functools.partial(attend_kernel, units), out_shape=jax.Sha...  83 us

profile of v6, /device:TPU:48, one launch (start us, length us, event | category | flops | bytes accessed | tf_op | source)
XLA Modules:
  0.0 84.7 jit_solution(15805805051499519467)
XLA Ops:
  0.0 83.0 %attend.1 = bf16[2,128,512]{2,1,0:T(8,128)(2,1)} custom-call(s32[2,4]{1,0:T(2,128)} %bitcast.1, s32[4]{0:T(128)} %prompts.1, s32[16]{0:T(128)} %tiles.1, bf16[1,128,1024]{2,1,0:T(8,128)(2,1)} %q.1, bf16[1,128,128]{2,1,0:T(8,128)(2,1)} %ck.1, bf16[1,128,128]{2,1,0:T(8,128)(2,1)} %cv.1, bf16[2,1024,128]{2,1,0:T(8,128)(2,1)} %pk.1, bf16[2,1024,128]{2,1,0:T(8,128)(2,1)} %pv.1, ...), custom_call_target="tpu_custom_call" | custom-call | tf_op jit(solution)/shard_map/attend/pallas_call | solution.py:506
  83.0 1.7 %copy.11 = bf16[2,128,512]{2,1,0:T(8,128)(2,1)} copy(bf16[2,128,512]{2,1,0:T(8,128)(2,1)} %attend.1) | data formatting | bytes 524288

commit v7 on v6

--- a/solution.py
+++ b/solution.py
@@ -53,7 +53,7 @@
     out,
     kall, vall, ckb, cvb, qbuf, obuf, rbuf, lob, lrb, sa, sb, ma, mb, low_a, low_b, sums_a, sums_b, acc_a, acc_b, info,
     wbuf, abuf, pbuf, far_in, leaf_in, inter_in, zin, zout, fin, xout,
-    load_sem, kv_send, kv_recv, q_send, q_recv, o_send, o_recv, l_send, l_recv,
+    load_sem, kv_send, kv_recv, q_send, q_recv, o_send, o_recv, l_send,
     a_send, a_recv, far_recv, leaf_recv, inter_recv, z_recv, f_send, x_send, x_recv,
 ):
     me = lax.axis_index("seq")
@@ -154,7 +154,7 @@
         k, j = at(place, u, units), slot * units + u
         return (
             remote(obuf.at[k], rbuf.at[j], o_send.at[0], o_recv.at[j], to),
-            remote(lob.at[k], lrb.at[j], l_send.at[0], l_recv.at[j], to),
+            remote(lob.at[k], lrb.at[j], l_send.at[0], o_recv.at[j], to),
         )
 
     def send_out(number, u, place, slot, to):
@@ -165,8 +165,8 @@
         k = at(place, u, units)
         js = [slot * units + u for slot in slots]
         for j in js:
-            wait_in(rbuf, o_recv, j)
-            wait_in(lrb, l_recv, j)
+            both_bytes = lob.at[pl.ds(0, 17)]
+            pltpu.make_async_copy(both_bytes, both_bytes, o_recv.at[j]).wait()
         logs = [lob[k]] + [lrb[j] for j in js]
         peak = functools.reduce(jnp.maximum, logs)
         weights = [jnp.exp2(x - peak) for x in logs]
@@ -249,9 +249,9 @@
         a_copy(5, u, T3, T5, bwd).start()
         if u >= units // 2:
             a_copy(1, u, T0, T2, bwd).start()
-        a_copy(4, u, T3, T4, fwd).start()
         wait_in(abuf, a_recv, T1 * units + u)
         a_copy(3, u, T1, T6, fwd).start()
+        a_copy(4, u, T3, T4, fwd).start()
 
     def a_relay2(u):
         wait_in(abuf, a_recv, T6 * units + u)
@@ -547,7 +547,6 @@
             dma((1,)),
             dma((7 * units,)),
             dma((1,)),
-            dma((7 * units,)),
             dma((1,)),
             dma((8 * units,)),
             dma((2 * PIECES,)),

time: 85.1 us -> 84.3 us (level)
  no operation moved by 1% of the time
where the time goes in v7:
time: 84.3 us; the launch traced here: 84.1 us
  Pallas kernels  82.5 us (98%)
  local copies, waits for them, and re-layouts  1.67 us (2%)
    pallas_call x1, Pallas kernels, attend(): pl.pallas_call(functools.partial(attend_kernel, units), out_shape=jax.Sha...  82.5 us

profile of v7, /device:TPU:48, one launch (start us, length us, event | category | flops | bytes accessed | tf_op | source)
XLA Modules:
  0.0 84.1 jit_solution(3758381092281819278)
XLA Ops:
  0.0 82.5 %attend.1 = bf16[2,128,512]{2,1,0:T(8,128)(2,1)} custom-call(s32[2,4]{1,0:T(2,128)} %bitcast.1, s32[4]{0:T(128)} %prompts.1, s32[16]{0:T(128)} %tiles.1, bf16[1,128,1024]{2,1,0:T(8,128)(2,1)} %q.1, bf16[1,128,128]{2,1,0:T(8,128)(2,1)} %ck.1, bf16[1,128,128]{2,1,0:T(8,128)(2,1)} %cv.1, bf16[2,1024,128]{2,1,0:T(8,128)(2,1)} %pk.1, bf16[2,1024,128]{2,1,0:T(8,128)(2,1)} %pv.1, ...), custom_call_target="tpu_custom_call" | custom-call | tf_op jit(solution)/shard_map/attend/pallas_call | solution.py:506
  82.5 1.7 %copy.11 = bf16[2,128,512]{2,1,0:T(8,128)(2,1)} copy(bf16[2,128,512]{2,1,0:T(8,128)(2,1)} %attend.1) | data formatting | bytes 524288
